TPU v7x, 32 devices: a whole 2x2x4 slice. The times are simulated.
32 devices in a mesh: slab: 4 (over z), pencil: 8 (over y, x, core).
Axes of the slice: x: 2, y: 2, z: 4, core: 2. Of those that a mesh axis runs over, the one named last changes fastest.
Arguments:
- right_sides: float32 [8, 128, 128, 128], P(None, 'slab', 'pencil'), may hold values from -6 to 6
- spectrum: float32 [128, 128, 128], P('pencil', 'slab'), may hold values from 0.5 to 20, as said below
- noise_var: float32 [128, 128, 128], P('slab', 'pencil'), may hold values from 0.05 to 1
- observed: int32 [128, 128, 128], P('slab', 'pencil'), may hold values 0 or 1
Outputs:
- solution: float32 [8, 128, 128, 128], P(None, 'slab', 'pencil')
- noise_grad: float32 [128, 128, 128], P('slab', 'pencil')
Inputs may be any that keep to these rules, and one draw needn't show every extreme that they name: Even in every index: spectrum[a, b, c] equals spectrum[(-a) mod 128, (-b) mod 128, (-c) mod 128].
All inputs are finite; a program needn't handle non-finite values. No bound on the sum of `observed` on one device may be relied on, other than what follows from the above.
Results may differ from a plain program's by a relative error of at most 0.00021.
Values sent between devices are 32-bit elements; how exact they have to be, the bound alone decides.
A program may use at most 128 MiB of HBM per device.

v0:
```python
import functools

import jax
import jax.numpy as jnp
import numpy as np
from jax import lax
from jax.experimental import pallas as pl
from jax.experimental.pallas import tpu as pltpu
from jax.sharding import PartitionSpec as P

ITERS = 3
SHIFT = 8.0
SCALE = 8.0
FLOOR = 3e-3
F32 = jnp.float32
BF16 = jnp.bfloat16
INTERPRET = False

precise = lax.Precision.HIGHEST


def embed(length, forward, scale=1.0):
    points = np.arange(length)
    angles = (points[:, None] * points[None, :] % length) * (2.0 * np.pi / length)
    cosine, sine = np.cos(angles) * scale, np.sin(angles) * scale
    if not forward:
        sine = -sine
    return np.block([[cosine, sine], [-sine, cosine]])


def halves(table):
    table = np.asarray(table, np.float32)
    high = table.astype(BF16)
    low = (table - high.astype(np.float32)).astype(BF16)
    return np.stack((high, low))


def split(values):
    high = values.astype(BF16)
    return high, (values - high.astype(F32)).astype(BF16)


def dot3(left, right, dims=((1,), (0,))):
    mul = functools.partial(
        lax.dot_general, dimension_numbers=(dims, ((), ())), preferred_element_type=F32
    )
    return mul(left[0], right[0]) + (mul(left[1], right[0]) + mul(left[0], right[1]))


def pair_of(ref):
    return ref[0], ref[1]


def forward_planes(planes, fx, fz):
    found = []
    for real, imag in planes:
        length = real.shape[1]
        first = dot3(fx, split(jnp.concatenate((real, imag), axis=1)), ((1,), (1,)))
        first = jnp.concatenate((first[:length], first[length:]), axis=1)
        found.append(dot3(split(first), fz))
    return jnp.swapaxes(jnp.stack(found), 0, 1)


def inverse_planes(values, gx, gz):
    rows = jnp.swapaxes(values, 0, 1)
    found = []
    for y in range(rows.shape[0]):
        first = dot3(split(rows[y]), gz)
        length = first.shape[1] // 2
        first = jnp.concatenate((first[:, :length], first[:, length:]), axis=0)
        plane = dot3(split(first), gx, ((0,), (0,)))
        width = plane.shape[1] // 2
        found.append((plane[:, :width], plane[:, width:]))
    return found


def planes_of(ref, y):
    count = ref.shape[0]
    return tuple(
        jnp.concatenate([ref[s, y, c] for s in range(count)], axis=0) for c in range(2)
    )


def lines_of(ref, y):
    return jnp.concatenate([ref[s, y] for s in range(ref.shape[0])], axis=0)


def first_kernel(w_ref, fx, fz, o_ref):
    planes = [planes_of(w_ref, y) for y in range(w_ref.shape[1])]
    o_ref[...] = forward_planes(planes, pair_of(fx), pair_of(fz))


def middle_kernel(d_ref, e_ref, fy, gy, o_ref):
    fy, gy = pair_of(fy), pair_of(gy)
    for a in range(d_ref.shape[1]):
        data = d_ref[:, a]
        data = data.reshape(-1, data.shape[-1])
        width = data.shape[1] // 2
        data = jnp.concatenate((data[:, :width], data[:, width:]), axis=0)
        spec = dot3(fy, split(data))
        eigen = e_ref[:, a].reshape(-1, e_ref.shape[-1])
        spec = spec * jnp.concatenate((eigen, eigen), axis=0)
        back = dot3(gy, split(spec))
        length = back.shape[0] // 2
        back = jnp.concatenate((back[:length], back[length:]), axis=1)
        o_ref[:, a] = back.reshape(o_ref.shape[0], o_ref.shape[2], o_ref.shape[3])


def next_kernel(u_ref, w_ref, n_ref, s_ref, gx, gz, fx, fz, w_out, o_ref):
    found = inverse_planes(u_ref[...], pair_of(gx), pair_of(gz))
    slabs, ys, _, depth, _ = w_ref.shape
    planes = []
    for y in range(ys):
        seen = lines_of(s_ref, y)
        noise = lines_of(n_ref, y) - SHIFT
        old = planes_of(w_ref, y)
        new = tuple((seen * t + noise * w) * (1.0 / SCALE) for t, w in zip(found[y], old))
        for s in range(slabs):
            for c in range(2):
                w_out[s, y, c] = new[c][s * depth : (s + 1) * depth]
        planes.append(new)
    o_ref[...] = forward_planes(planes, pair_of(fx), pair_of(fz))


def last_kernel(u_ref, gx, gz, w_out):
    found = inverse_planes(u_ref[...], pair_of(gx), pair_of(gz))
    slabs, ys, _, depth, _ = w_out.shape
    for y in range(ys):
        for s in range(slabs):
            for c in range(2):
                w_out[s, y, c] = found[y][c][s * depth : (s + 1) * depth]


def whole(shape):
    return pl.BlockSpec(shape, lambda i: (0,) * len(shape))


def along(shape, axis, block):
    full = tuple(block if d == axis else n for d, n in enumerate(shape))
    return pl.BlockSpec(full, lambda i: tuple(i if d == axis else 0 for d in range(len(shape))))


def call(kernel, args, specs, outs, out_specs, steps, flops=0):
    many = isinstance(outs, (list, tuple))
    return pl.pallas_call(
        kernel,
        grid=(steps,),
        in_specs=specs,
        out_specs=out_specs,
        out_shape=outs,
        interpret=INTERPRET,
        cost_estimate=pl.CostEstimate(
            flops=flops, bytes_accessed=sum(a.size * 4 for a in args), transcendentals=0
        ),
        compiler_params=pltpu.CompilerParams(vmem_limit_bytes=56 * 2**20),
    )(*args)


def gram_kernel(l_ref, r_ref, o_ref):
    quads, ys, both, depth, _ = l_ref.shape
    columns = quads * both
    tile = min(8, depth)
    index = [(i, j) for i in range(columns) for j in range(i, columns)]

    def load(ref, y, z):
        return [ref[i // both, y, i % both, pl.ds(z, tile)] for i in range(columns)]

    def body(step, sums):
        y = step // (depth // tile)
        z = pl.multiple_of(step % (depth // tile) * tile, tile)
        left, right = load(l_ref, y, z), load(r_ref, y, z)
        return tuple(s + left[i] * right[j] for s, (i, j) in zip(sums, index))

    zero = jnp.zeros((tile, l_ref.shape[-1]), F32)
    sums = lax.fori_loop(0, ys * (depth // tile), body, (zero,) * len(index))
    for total, (i, j) in zip(sums, index):
        row = jnp.sum(total, axis=0, keepdims=True)
        o_ref[pl.ds(i * columns + j, 1)] = row
        if i != j:
            o_ref[pl.ds(j * columns + i, 1)] = row


def moment(left, right):
    columns = left.shape[0] * left.shape[2]
    rows = pl.pallas_call(
        gram_kernel,
        out_shape=jax.ShapeDtypeStruct((columns * columns, left.shape[-1]), F32),
        interpret=INTERPRET,
        cost_estimate=pl.CostEstimate(
            flops=left.size * columns, bytes_accessed=left.size * 8, transcendentals=0
        ),
    )(left, right)
    return jnp.sum(rows, axis=1)


def solve(matrix, right_hand):
    size = matrix.shape[0]
    both = jnp.concatenate((0.5 * (matrix + matrix.T), right_hand), axis=1)
    place = lax.broadcasted_iota(jnp.int32, both.shape, 0)
    for i in range(size):
        row = both[i : i + 1] / both[i : i + 1, i : i + 1]
        both = jnp.where(place == i, row, both - both[:, i : i + 1] * row)
    return both[:, size:]


def least_pivots(matrix):
    size = matrix.shape[0]
    both = 0.5 * (matrix + matrix.T)
    place = lax.broadcasted_iota(jnp.int32, both.shape, 0)
    lane = lax.broadcasted_iota(jnp.int32, both.shape, 1)
    for i in range(size):
        row = both[i : i + 1] / both[i : i + 1, i : i + 1]
        both = jnp.where(place > i, both - both[:, i : i + 1] * row, both)
    return jnp.sum(jnp.where(place == lane, both, 0.0), axis=0, keepdims=True)


def dot(left, right):
    return jnp.dot(left, right, precision=precise, preferred_element_type=F32)


def small_kernel(h_ref, c_ref, ok_ref):
    hankel = h_ref[...]
    columns = hankel.shape[0] // (ITERS + 1)

    def operator(c):
        zero = jnp.zeros((columns, columns), F32)
        return SHIFT * c + SCALE * jnp.concatenate((zero, c[: ITERS * columns]), axis=0)

    def inner(u, v):
        return dot(u.T, dot(hankel, v))

    shape = (hankel.shape[0], columns)
    same = lax.broadcasted_iota(jnp.int32, shape, 0) == lax.broadcasted_iota(jnp.int32, shape, 1)
    residual = jnp.where(same, 1.0, 0.0).astype(F32)
    direction, answer = residual, jnp.zeros(shape, F32)
    gamma = hankel[:columns, :columns]
    start = least_pivots(gamma)
    fine = jnp.ones((1, columns), F32)
    for iteration in range(ITERS):
        image = operator(direction)
        alpha = solve(inner(direction, image), gamma)
        answer = answer + dot(direction, alpha)
        if iteration + 1 < ITERS:
            residual = residual - dot(image, alpha)
            gamma_next = inner(residual, residual)
            fine = jnp.where(least_pivots(gamma_next) > FLOOR * start, fine, 0.0)
            beta = solve(gamma, gamma_next)
            direction = residual + dot(direction, beta)
            gamma = gamma_next
    c_ref[...] = answer
    ok_ref[...] = fine


def final_kernel(c_ref, p0, p1, p2, x_ref, g_ref):
    quads, ys, both, depth, _ = p0.shape
    columns = quads * both
    tile = min(8, depth)
    basis = (p0, p1, p2)
    for half in range(2):
        span = range(half * columns // 2, (half + 1) * columns // 2)
        mix = [[c_ref[k * columns + i, p] for p in span] for k in range(3) for i in range(columns)]

        def body(step, carry):
            y = step // (depth // tile)
            rows = pl.ds(pl.multiple_of(step % (depth // tile) * tile, tile), tile)
            sums = [0.0] * len(span)
            for k in range(3):
                for i in range(columns):
                    value = basis[k][i // both, y, i % both, rows]
                    sums = [s + value * m for s, m in zip(sums, mix[k * columns + i])]
            grad = 0.0
            for s, p in zip(sums, span):
                x_ref[p // both, y, p % both, rows] = s
                if p == 0:
                    grad = grad + 0.5 * s * s
                else:
                    grad = grad - p0[p // both, y, p % both, rows] * s * (0.5 / (columns - 1))
            g_ref[y, rows] = grad if half == 0 else g_ref[y, rows] + grad
            return carry

        lax.fori_loop(0, ys * (depth // tile), body, 0)


def travel_kernel(plan, sizes, *refs):
    count = len(plan)
    sources, targets = refs[:count], refs[count : 2 * count]
    send_sem, recv_sem, own_sem = refs[2 * count :]
    axes = tuple(dict.fromkeys(axis for axis, _ in plan))
    place = {axis: lax.axis_index(axis) for axis in sizes}
    barrier = pltpu.get_barrier_semaphore()

    def peer(axis, step):
        other = lax.rem(place[axis] + step, sizes[axis])
        return tuple(other if name == axis else place[name] for name in sizes)

    total = 0
    for axis in axes:
        for step in range(1, sizes[axis]):
            pl.semaphore_signal(
                barrier, inc=1, device_id=peer(axis, step), device_id_type=pl.DeviceIdType.MESH
            )
            total += 1
    pl.semaphore_wait(barrier, total)
    copies = []
    slot = 0
    order = []
    for number, (axis, gather) in enumerate(plan):
        for step in range(1, sizes[axis]):
            order.append((abs(2 * step - sizes[axis]), number, step, slot))
            slot += 1
    for _, number, step, slot in sorted(order):
        axis, gather = plan[number]
        other = lax.rem(place[axis] + step, sizes[axis])
        source = sources[number] if gather else sources[number].at[other]
        copy = pltpu.make_async_remote_copy(
            src_ref=source,
            dst_ref=targets[number].at[place[axis]],
            send_sem=send_sem.at[slot],
            recv_sem=recv_sem.at[slot],
            device_id=peer(axis, step),
            device_id_type=pl.DeviceIdType.MESH,
        )
        copy.start()
        copies.append(copy)
    for number, (axis, gather) in enumerate(plan):
        source = sources[number] if gather else sources[number].at[place[axis]]
        copy = pltpu.make_async_copy(
            source, targets[number].at[place[axis]], own_sem.at[number]
        )
        copy.start()
        copies.append(copy)
    for copy in copies:
        copy.wait()


def travel(identity, *moves):
    sizes = {name: lax.axis_size(name) for name in ("slab", "pencil")}
    plan = tuple((axis, gather) for _, axis, gather in moves)
    arrays = [array for array, _, _ in moves]
    slots = sum(sizes[axis] - 1 for axis, _ in plan)
    outs = tuple(
        jax.ShapeDtypeStruct(((sizes[axis],) if gather else ()) + array.shape, array.dtype)
        for array, axis, gather in moves
    )
    if INTERPRET:
        found = [
            lax.all_gather(v, axis) if gather else lax.all_to_all(v, axis, 0, 0, tiled=True)
            for v, axis, gather in moves
        ]
        return found
    return pl.pallas_call(
        functools.partial(travel_kernel, plan, sizes),
        in_specs=[pl.BlockSpec(memory_space=pltpu.VMEM)] * len(arrays),
        out_specs=(pl.BlockSpec(memory_space=pltpu.VMEM),) * len(arrays),
        out_shape=outs,
        scratch_shapes=[
            pltpu.SemaphoreType.DMA((slots,)),
            pltpu.SemaphoreType.DMA((slots,)),
            pltpu.SemaphoreType.DMA((len(arrays),)),
        ],
        cost_estimate=pl.CostEstimate(flops=0, bytes_accessed=2**26, transcendentals=0),
        compiler_params=pltpu.CompilerParams(collective_id=identity, has_side_effects=True),
    )(*arrays)


def recurrences(p0, p1, p2, u2):
    flat = lambda v: jnp.swapaxes(v, 1, 2).reshape(v.shape[0] * v.shape[2], -1)
    basis = [flat(v) for v in (p0, p1, p2, u2)]
    shape = (p0.shape[0], p0.shape[2], p0.shape[1]) + p0.shape[3:]
    columns = basis[0].shape[0]

    def field(c):
        return sum(dot(c[k].T, basis[k]) for k in range(len(c)))

    def gram(u, v):
        local_sum = jnp.dot(u, v.T, precision=precise)
        return lax.psum(local_sum, ("slab", "pencil"))

    def operator(c):
        zero = jnp.zeros((1, columns, columns), F32)
        return SHIFT * jnp.concatenate((c, zero)) + SCALE * jnp.concatenate((zero, c))

    def longer(c):
        return jnp.concatenate((c, jnp.zeros((1, columns, columns), F32)))

    residual = direction = answer = jnp.eye(columns, dtype=F32)[None]
    answer = 0.0 * answer
    vector = field(residual)
    gamma = gram(vector, vector)
    for iteration in range(ITERS):
        image = operator(direction)
        alpha = solve(gram(field(direction), field(image)), gamma)
        answer = answer + jnp.einsum("kij,jp->kip", direction, alpha, precision=precise)
        if iteration + 1 < ITERS:
            residual = longer(residual) - jnp.einsum("kij,jp->kip", image, alpha, precision=precise)
            vector = field(residual)
            gamma_next = gram(vector, vector)
            beta = solve(gamma, gamma_next)
            direction = residual + longer(
                jnp.einsum("kij,jp->kip", direction, beta, precision=precise)
            )
            answer = longer(answer)
            gamma = gamma_next
    return answer.reshape(-1, columns)


def local(right_sides, spectrum, noise_var, observed):
    columns, depth, ys, nx = right_sides.shape
    slabs, pencils = lax.axis_size("slab"), lax.axis_size("pencil")
    nz, ny = depth * slabs, ys * pencils
    seen = jnp.swapaxes(observed.astype(F32), 0, 1)
    noise = jnp.swapaxes(noise_var, 0, 1)
    field = jnp.transpose(right_sides.reshape(columns // 2, 2, depth, ys, nx), (0, 3, 1, 2, 4))

    own = columns // slabs
    quads = columns // 2

    def to_planes(values):
        if own % 2:
            values = jnp.swapaxes(values, 1, 2).reshape(columns, ys, 1, depth, nx)
            values = jnp.concatenate((values, jnp.zeros_like(values)), axis=2)
        return travel(0, (values, "slab", False))[0]

    def from_planes(values):
        if own % 2:
            values = values[:, :, 0].reshape(quads, 2, ys, depth, nx)
            values = jnp.swapaxes(values, 1, 2)
        return values

    fx, gx = halves(embed(nx, True)), halves(embed(nx, False).T)
    fz, gz = halves(embed(nz, True).T), halves(embed(nz, False).T)
    fy, gy = halves(embed(ny, True)), halves(embed(ny, False, 1.0 / (nx * ny * nz)))
    fx, gx, fz, gz, fy, gy = (jnp.asarray(t) for t in (fx, gx, fz, gz, fy, gy))

    part = nx // pencils
    chunk = 8 if ys % 8 == 0 else ys
    wide = 2 * nz
    tables = lambda *ts: [whole(t.shape) for t in ts]
    sent_shape = (nx, ys, wide)
    work = 12 * 2 * ys * nx * nz * 2 * (nx + nz)

    w0 = to_planes(field * seen[None, :, None])
    shape = w0.shape
    w_spec = along(shape, 1, chunk)
    sent_spec = along(sent_shape, 1, chunk)
    steps = ys // chunk
    sent = call(
        first_kernel, (w0, fx, fz), [w_spec] + tables(fx, fz),
        jax.ShapeDtypeStruct(sent_shape, F32), sent_spec, steps, work,
    )
    m_spec = along((slabs, ys, depth, nx), 1, chunk)

    def blocks(sent):
        return sent.reshape(pencils, part, ys, wide), "pencil", False

    def middle(got, eigen):
        if ys % 8:
            got = jnp.swapaxes(got, 0, 1).reshape(1, part, ny, wide)
        if eigen.shape[2] % 8:
            eigen = jnp.swapaxes(eigen, 0, 1).reshape(1, part, ny, nz)
        block = min(4, part)
        back = call(
            middle_kernel, (got, eigen, fy, gy),
            [along(got.shape, 1, block), along(eigen.shape, 1, block)] + tables(fy, gy),
            jax.ShapeDtypeStruct(got.shape, F32), along(got.shape, 1, block), part // block, work,
        )
        if ys % 8:
            back = jnp.swapaxes(back.reshape(part, pencils, ys, wide), 0, 1)
        return back, "pencil", False

    def advance(w, got):
        return call(
            next_kernel, (got.reshape(sent_shape), w, noise_all, seen_all, gx, gz, fx, fz),
            [sent_spec, w_spec, m_spec, m_spec] + tables(gx, gz, fx, fz),
            (jax.ShapeDtypeStruct(shape, F32), jax.ShapeDtypeStruct(sent_shape, F32)),
            (w_spec, sent_spec), steps, 2 * work,
        )

    got, eigen = travel(1, blocks(sent), (spectrum, "slab", True))
    got, noise_all, seen_all = travel(
        2, middle(got, eigen), (noise, "slab", True), (seen, "slab", True)
    )
    plane, sent = advance(w0, got)
    got, low = travel(3, blocks(sent), (plane[:, : ys // 2], "slab", False))
    got, high = travel(4, middle(got, eigen), (plane[:, ys // 2 :], "slab", False))
    w1 = jnp.concatenate((low, high), axis=1)
    w2, sent = advance(plane, got)
    got, low = travel(5, blocks(sent), (w2[:, : ys // 2], "slab", False))
    got, high = travel(6, middle(got, eigen), (w2[:, ys // 2 :], "slab", False))
    w2 = jnp.concatenate((low, high), axis=1)
    t3 = call(
        last_kernel, (got.reshape(sent_shape), gx, gz), [sent_spec] + tables(gx, gz),
        jax.ShapeDtypeStruct(shape, F32), w_spec, steps, work,
    )
    (t3,) = travel(7, (t3, "slab", False))

    seen_here, factor = seen[None, :, None], ((noise - SHIFT) * (1.0 / SCALE))[None, :, None]
    p0 = field
    p1 = jnp.where(seen_here > 0, from_planes(w1), factor * p0)
    p2 = jnp.where(seen_here > 0, from_planes(w2), factor * (factor * p0))
    u2 = (1.0 / SCALE) * seen_here * from_planes(t3) + factor * p2
    sums = [moment(l, r) for l, r in ((p0, p0), (p0, p1), (p1, p1), (p1, p2), (p2, p2), (p2, u2))]
    zeros = jnp.zeros((2, columns * columns), F32)
    (sums,) = travel(8, (jnp.concatenate((jnp.stack(sums), zeros)), "pencil", True))
    (sums,) = travel(9, (jnp.sum(sums, axis=0), "slab", True))
    sums = jnp.sum(sums, axis=0)[:6]
    sums = [s.reshape(columns, columns) for s in sums] + [jnp.zeros((columns, columns), F32)]
    hankel = jnp.concatenate(
        [jnp.concatenate([sums[min(j + k, 6)] for k in range(4)], axis=1) for j in range(4)], axis=0
    )
    coefficients, fine = pl.pallas_call(
        small_kernel,
        out_shape=(
            jax.ShapeDtypeStruct((4 * columns, columns), F32),
            jax.ShapeDtypeStruct((1, columns), F32),
        ),
        interpret=INTERPRET,
    )(hankel)
    coefficients = lax.cond(
        jnp.min(fine) > 0.5,
        lambda: coefficients[: 3 * columns],
        lambda: recurrences(p0, p1, p2, u2),
    )
    answer, grad = pl.pallas_call(
        final_kernel,
        in_specs=[pl.BlockSpec(memory_space=pltpu.SMEM)]
        + [pl.BlockSpec(memory_space=pltpu.VMEM)] * 3,
        out_shape=(
            jax.ShapeDtypeStruct(field.shape, F32),
            jax.ShapeDtypeStruct((ys, depth, nx), F32),
        ),
        interpret=INTERPRET,
    )(coefficients, p0, p1, p2)
    answer = jnp.transpose(answer, (0, 2, 3, 1, 4)).reshape(columns, depth, ys, nx)
    return answer, jnp.swapaxes(grad, 0, 1)


def solution(mesh):
    in_specs = (
        P(None, "slab", "pencil", None),
        P("pencil", "slab", None),
        P("slab", "pencil", None),
        P("slab", "pencil", None),
    )
    out_specs = (P(None, "slab", "pencil", None), P("slab", "pencil", None))
    return jax.shard_map(local, mesh=mesh, in_specs=in_specs, out_specs=out_specs, check_vma=False)
```

profile of v0, /device:TPU:0, one launch (start us, length us, event | category | flops | bytes accessed | tf_op | source)
XLA Modules:
  0.0 468.3 jit_solution(7782728609154789682)
XLA Ops:
  8.7 42.7 %shard_map.114.w_ref = f32[4,16,2,32,128]{4,3,2,1,0:T(8,128)} custom-call(f32[4,16,2,32,128]{4,3,2,1,0:T(8,128)} %broadcast_multiply_fusion.refs_0_), custom_call_target="tpu_custom_call" | custom-call | bytes 67108864 | tf_op jit(solution)/shard_map/pallas_call | solution.py:351
  51.4 9.1 %shard_map.115 = f32[128,16,256]{2,1,0:T(8,128)} custom-call(f32[4,16,2,32,128]{4,3,2,1,0:T(8,128)} %shard_map.114.w_ref, bf16[2,256,256]{2,1,0:T(8,128)(2,1)} %constant.15.clone.fx.fy.gx.gz, bf16[2,256,256]{2,1,0:T(8,128)(2,1)} %constant.16.clone.fz), custom_call_target="tpu_custom_call" | custom-call | flops 3221225472 | bytes 3145728 | tf_op jit(solution)/shard_map/pallas_call | solution.py:145
  60.5 39.0 %shard_map.116 = (f32[8,16,16,256]{3,2,1,0:T(8,128)}, f32[4,16,32,128]{3,2,1,0:T(8,128)}) custom-call(f32[8,16,16,256]{3,2,1,0:T(8,128)} %bitcast.319, f32[16,32,128]{2,1,0:T(8,128)} %refs_1_.1), custom_call_target="tpu_custom_call" | custom-call | bytes 67108864 | tf_op jit(solution)/shard_map/pallas_call | solution.py:351
  99.5 8.6 %shard_map.117.refs_0_ = f32[8,16,16,256]{3,2,1,0:T(8,128)} custom-call(f32[8,16,16,256]{3,2,1,0:T(8,128)} %get-tuple-element.39.d_ref, f32[4,16,32,128]{3,2,1,0:T(8,128)} %get-tuple-element.40.e_ref, bf16[2,256,256]{2,1,0:T(8,128)(2,1)} %constant.15.clone.fx.fy.gx.gz, bf16[2,256,256]{2,1,0:T(8,128)(2,1)} %constant.17.clone.gy), custom_call_target="tpu_custom_call" | custom-call | flops 3221225472 | bytes 4194304 | tf_op jit(solution)/shard_map/pallas_call | solution.py:145
  108.1 43.3 %shard_map.118 = (f32[8,16,16,256]{3,2,1,0:T(8,128)}, f32[4,16,32,128]{3,2,1,0:T(8,128)}, f32[4,16,32,128]{3,2,1,0:T(8,128)}) custom-call(f32[8,16,16,256]{3,2,1,0:T(8,128)} %shard_map.117.refs_0_, f32[16,32,128]{2,1,0:T(8,128)} %bitcast.322, f32[16,32,128]{2,1,0:T(8,128)} %copy-done.13), custom_call_target="tpu_custom_call" | custom-call | bytes 67108864 | tf_op jit(solution)/shard_map/pallas_call | solution.py:351
  151.4 13.0 %shard_map.119 = (f32[4,16,2,32,128]{4,3,2,1,0:T(8,128)}, f32[128,16,256]{2,1,0:T(8,128)}) custom-call(f32[128,16,256]{2,1,0:T(8,128)} %bitcast.331, f32[4,16,2,32,128]{4,3,2,1,0:T(8,128)} %shard_map.114.w_ref, f32[4,16,32,128]{3,2,1,0:T(8,128)} %get-tuple-element.42.n_ref, f32[4,16,32,128]{3,2,1,0:T(8,128)} %get-tuple-element.43.s_ref, ...), custom_call_target="tpu_custom_call" | custom-call | flops 6442450944 | bytes 8388608 | tf_op jit(solution)/shard_map/pallas_call | solution.py:145
  166.3 4.8 %shard_map.113 = f32[64,128]{1,0:T(8,128)} custom-call(f32[4,16,2,32,128]{4,3,2,1,0:T(8,128)} %bitcast.307, f32[4,16,2,32,128]{4,3,2,1,0:T(8,128)} %bitcast.308), custom_call_target="tpu_custom_call" | custom-call | flops 4194304 | bytes 4194304 | tf_op jit(solution)/shard_map/pallas_call | solution.py:185
  173.7 39.6 %shard_map.120 = (f32[8,16,16,256]{3,2,1,0:T(8,128)}, f32[4,8,2,32,128]{4,3,2,1,0:T(8,128)}) custom-call(f32[8,16,16,256]{3,2,1,0:T(8,128)} %bitcast.317, f32[4,8,2,32,128]{4,3,2,1,0:T(8,128)} %get-tuple-element.88.refs_1_), custom_call_target="tpu_custom_call" | custom-call | bytes 67108864 | tf_op jit(solution)/shard_map/pallas_call | solution.py:351
  213.3 8.6 %shard_map.121.refs_0_ = f32[8,16,16,256]{3,2,1,0:T(8,128)} custom-call(f32[8,16,16,256]{3,2,1,0:T(8,128)} %get-tuple-element.47.d_ref, f32[4,16,32,128]{3,2,1,0:T(8,128)} %get-tuple-element.40.e_ref, bf16[2,256,256]{2,1,0:T(8,128)(2,1)} %constant.15.clone.fx.fy.gx.gz, bf16[2,256,256]{2,1,0:T(8,128)(2,1)} %constant.17.clone.gy), custom_call_target="tpu_custom_call" | custom-call | flops 3221225472 | bytes 4194304 | tf_op jit(solution)/shard_map/pallas_call | solution.py:145
  221.9 30.4 %shard_map.122 = (f32[8,16,16,256]{3,2,1,0:T(8,128)}, f32[4,8,2,32,128]{4,3,2,1,0:T(8,128)}) custom-call(f32[8,16,16,256]{3,2,1,0:T(8,128)} %shard_map.121.refs_0_, f32[4,8,2,32,128]{4,3,2,1,0:T(8,128)} %get-tuple-element.87.refs_1_), custom_call_target="tpu_custom_call" | custom-call | bytes 67108864 | tf_op jit(solution)/shard_map/pallas_call | solution.py:351
  252.3 13.2 %shard_map.125 = (f32[4,16,2,32,128]{4,3,2,1,0:T(8,128)}, f32[128,16,256]{2,1,0:T(8,128)}) custom-call(f32[128,16,256]{2,1,0:T(8,128)} %bitcast.330, f32[4,16,2,32,128]{4,3,2,1,0:T(8,128)} %get-tuple-element.45.w_ref, f32[4,16,32,128]{3,2,1,0:T(8,128)} %get-tuple-element.42.n_ref, f32[4,16,32,128]{3,2,1,0:T(8,128)} %get-tuple-element.43.s_ref, ...), custom_call_target="tpu_custom_call" | custom-call | flops 6442450944 | bytes 8388608 | tf_op jit(solution)/shard_map/pallas_call | solution.py:145
  268.6 29.9 %shard_map.126 = (f32[8,16,16,256]{3,2,1,0:T(8,128)}, f32[4,8,2,32,128]{4,3,2,1,0:T(8,128)}) custom-call(f32[8,16,16,256]{3,2,1,0:T(8,128)} %bitcast.318, f32[4,8,2,32,128]{4,3,2,1,0:T(8,128)} %get-tuple-element.86.refs_1_), custom_call_target="tpu_custom_call" | custom-call | bytes 67108864 | tf_op jit(solution)/shard_map/pallas_call | solution.py:351
  298.6 8.6 %shard_map.127.refs_0_ = f32[8,16,16,256]{3,2,1,0:T(8,128)} custom-call(f32[8,16,16,256]{3,2,1,0:T(8,128)} %get-tuple-element.53.d_ref, f32[4,16,32,128]{3,2,1,0:T(8,128)} %get-tuple-element.40.e_ref, bf16[2,256,256]{2,1,0:T(8,128)(2,1)} %constant.15.clone.fx.fy.gx.gz, bf16[2,256,256]{2,1,0:T(8,128)(2,1)} %constant.17.clone.gy), custom_call_target="tpu_custom_call" | custom-call | flops 3221225472 | bytes 4194304 | tf_op jit(solution)/shard_map/pallas_call | solution.py:145
  307.1 30.6 %shard_map.128 = (f32[8,16,16,256]{3,2,1,0:T(8,128)}, f32[4,8,2,32,128]{4,3,2,1,0:T(8,128)}) custom-call(f32[8,16,16,256]{3,2,1,0:T(8,128)} %shard_map.127.refs_0_, f32[4,8,2,32,128]{4,3,2,1,0:T(8,128)} %get-tuple-element.85.refs_1_), custom_call_target="tpu_custom_call" | custom-call | bytes 67108864 | tf_op jit(solution)/shard_map/pallas_call | solution.py:351
  337.7 5.1 %shard_map.131.refs_0_ = f32[4,16,2,32,128]{4,3,2,1,0:T(8,128)} custom-call(f32[128,16,256]{2,1,0:T(8,128)} %bitcast.332, bf16[2,256,256]{2,1,0:T(8,128)(2,1)} %constant.15.clone.fx.fy.gx.gz, bf16[2,256,256]{2,1,0:T(8,128)(2,1)} %constant.15.clone.fx.fy.gx.gz), custom_call_target="tpu_custom_call" | custom-call | flops 3221225472 | bytes 3145728 | tf_op jit(solution)/shard_map/pallas_call | solution.py:145
  342.9 40.9 %shard_map.132 = f32[4,16,2,32,128]{4,3,2,1,0:T(8,128)} custom-call(f32[4,16,2,32,128]{4,3,2,1,0:T(8,128)} %shard_map.131.refs_0_), custom_call_target="tpu_custom_call" | custom-call | bytes 67108864 | tf_op jit(solution)/shard_map/pallas_call | solution.py:351
  383.8 6.8 %multiply_add_fusion = (f32[4,16,2,32,128]{4,3,2,1,0:T(8,128)}, f32[4,16,2,32,128]{4,3,2,1,0:T(8,128)S(1)}, f32[4,16,2,32,128]{4,3,2,1,0:T(8,128)}) fusion(f32[4,16,2,32,128]{4,3,2,1,0:T(8,128)} %shard_map.132, f32[16,32,128]{2,1,0:T(8,128)} %get-tuple-element.90, f32[16,32,128]{2,1,0:T(8,128)S(1)} %get-tuple-element.89, ...), kind=kLoop, calls=%fused_computation.220 | loop fusion | flops 4718592 | bytes 15269888 | tf_op jit(solution)/shard_map/add | solution.py:501
  390.6 4.7 %shard_map.133 = f32[64,128]{1,0:T(8,128)} custom-call(f32[4,16,2,32,128]{4,3,2,1,0:T(8,128)S(1)} %get-tuple-element.81.r_ref.l_ref.p2, f32[4,16,2,32,128]{4,3,2,1,0:T(8,128)} %get-tuple-element.80.r_ref), custom_call_target="tpu_custom_call" | custom-call | flops 4194304 | bytes 4194304 | tf_op jit(solution)/shard_map/pallas_call | solution.py:185
  404.3 4.6 shard_map.124
  409.8 4.6 shard_map.123
  415.9 6.0 %shard_map.134 = f32[8,8,64]{2,1,0:T(8,128)} custom-call(f32[8,64]{1,0:T(8,128)} %concatenate.75.refs_0_), custom_call_target="tpu_custom_call" | custom-call | bytes 67108864 | tf_op jit(solution)/shard_map/pallas_call | solution.py:351
  423.3 16.1 %shard_map.135 = f32[4,8,64]{2,1,0:T(8,128)} custom-call(f32[8,64]{1,0:T(8,128)} %reduce_sum.78.refs_0_), custom_call_target="tpu_custom_call" | custom-call | bytes 67108864 | tf_op jit(solution)/shard_map/pallas_call | solution.py:351
  441.4 7.5 %shard_map.136 = (f32[32,8]{1,0:T(8,128)S(1)}, f32[1,8]{1,0:T(1,128)}) custom-call(f32[32,32]{1,0:T(8,128)} %maximum_maximum_fusion.h_ref), custom_call_target="tpu_custom_call" | custom-call | tf_op jit(solution)/shard_map/pallas_call | solution.py:511
  451.0 12.2 %shard_map.137 = (f32[4,16,2,32,128]{4,3,2,1,0:T(8,128)}, f32[16,32,128]{2,1,0:T(8,128)}) custom-call(f32[24,8]{1,0:T(8,128)S(1)} %get-tuple-element.91.c_ref, f32[4,16,2,32,128]{4,3,2,1,0:T(8,128)} %bitcast.310, f32[4,16,2,32,128]{4,3,2,1,0:T(8,128)} %get-tuple-element.84.r_ref.l_ref.p1, f32[4,16,2,32,128]{4,3,2,1,0:T(8,128)} %copy-done.5), custom_call_target="tpu_custom_call" | custom-call | tf_op jit(solution)/shard_map/pallas_call | solution.py:524
  (46 shorter events, 36.9 us)
Async XLA Ops:
  0.6 6.0 %copy-start.10 = (f32[8,32,16,128]{3,2,1,0:T(8,128)S(1)}, f32[8,32,16,128]{3,2,1,0:T(8,128)}, u32[]{:S(2)}) copy-start(f32[8,32,16,128]{3,2,1,0:T(8,128)} %param.12) | copy-start | bytes 6291460
  2.9 5.8 %copy-start.13 = (f32[16,32,128]{2,1,0:T(8,128)}, f32[16,32,128]{2,1,0:T(8,128)S(1)}, u32[]{:S(2)}) copy-start(f32[16,32,128]{2,1,0:T(8,128)S(1)} %fusion.32.refs_2_) | copy-start | bytes 786436
  166.3 5.6 %copy-start.14 = (f32[4,16,2,32,128]{4,3,2,1,0:T(8,128)S(1)}, f32[4,16,2,32,128]{4,3,2,1,0:T(8,128)}, u32[]{:S(2)}) copy-start(f32[4,16,2,32,128]{4,3,2,1,0:T(8,128)} %get-tuple-element.45.w_ref) | copy-start | bytes 6291460
  342.9 40.9 %copy-start.15 = (f32[4,8,2,32,128]{4,3,2,1,0:T(8,128)S(1)}, f32[4,8,2,32,128]{4,3,2,1,0:T(8,128)}, u32[]{:S(2)}) copy-start(f32[4,8,2,32,128]{4,3,2,1,0:T(8,128)} %get-tuple-element.46) | copy-start | bytes 3145732
  390.6 60.1 %copy-start.5 = (f32[4,16,2,32,128]{4,3,2,1,0:T(8,128)}, f32[4,16,2,32,128]{4,3,2,1,0:T(8,128)S(1)}, u32[]{:S(2)}) copy-start(f32[4,16,2,32,128]{4,3,2,1,0:T(8,128)S(1)} %get-tuple-element.81.r_ref.l_ref.p2) | copy-start | bytes 6291460
  463.3 4.2 copy-start.16
where the time goes:
time: 470 us; the launch traced here: 468 us
  Pallas kernels  430 us (91%)
  other arithmetic  22.2 us (5%)
  local copies, waits for them, and re-layouts  14.8 us (3%)
    pallas_call x10, Pallas kernels, travel(): pl.pallas_call(functools.partial(travel_kernel, plan, sizes), in_specs=[p...  319 us
    pallas_call x7, Pallas kernels, call(): pl.pallas_call(kernel, grid=(steps,), in_specs=specs, out_specs=out_specs...  66.1 us
    pallas_call x6, Pallas kernels, moment(): pl.pallas_call(gram_kernel, out_shape=jax.ShapeDtypeStruct((columns * col...  25.2 us
    pallas_call x1, Pallas kernels, local(): pl.pallas_call(final_kernel, in_specs=[pl.BlockSpec(memory_space=pltpu.SM...  12.2 us

commit v1 on v0

v1 whole, which is shorter than its diff:
```python
import functools

import jax
import jax.numpy as jnp
import numpy as np
from jax import lax
from jax.experimental import pallas as pl
from jax.experimental.pallas import tpu as pltpu
from jax.sharding import PartitionSpec as P

ITERS = 3
SHIFT = 8.0
SCALE = 8.0
FLOOR = 3e-3
F32 = jnp.float32
BF16 = jnp.bfloat16
INTERPRET = False

precise = lax.Precision.HIGHEST


def embed(length, forward, scale=1.0):
    points = np.arange(length)
    angles = (points[:, None] * points[None, :] % length) * (2.0 * np.pi / length)
    cosine, sine = np.cos(angles) * scale, np.sin(angles) * scale
    if not forward:
        sine = -sine
    return np.block([[cosine, sine], [-sine, cosine]])


def halves(table):
    table = np.asarray(table, np.float32)
    high = table.astype(BF16)
    low = (table - high.astype(np.float32)).astype(BF16)
    return np.stack((high, low))


def split(values):
    high = values.astype(BF16)
    return high, (values - high.astype(F32)).astype(BF16)


def dot3(left, right, dims=((1,), (0,))):
    mul = functools.partial(
        lax.dot_general, dimension_numbers=(dims, ((), ())), preferred_element_type=F32
    )
    return mul(left[0], right[0]) + (mul(left[1], right[0]) + mul(left[0], right[1]))


def solve(matrix, right_hand):
    size = matrix.shape[0]
    both = jnp.concatenate((0.5 * (matrix + matrix.T), right_hand), axis=1)
    place = lax.broadcasted_iota(jnp.int32, both.shape, 0)
    for i in range(size):
        row = both[i : i + 1] / both[i : i + 1, i : i + 1]
        both = jnp.where(place == i, row, both - both[:, i : i + 1] * row)
    return both[:, size:]


def least_pivots(matrix):
    size = matrix.shape[0]
    both = 0.5 * (matrix + matrix.T)
    place = lax.broadcasted_iota(jnp.int32, both.shape, 0)
    lane = lax.broadcasted_iota(jnp.int32, both.shape, 1)
    for i in range(size):
        row = both[i : i + 1] / both[i : i + 1, i : i + 1]
        both = jnp.where(place > i, both - both[:, i : i + 1] * row, both)
    return jnp.sum(jnp.where(place == lane, both, 0.0), axis=0, keepdims=True)


def dot(left, right):
    return jnp.dot(left, right, precision=precise, preferred_element_type=F32)


def small(hankel):
    columns = hankel.shape[0] // (ITERS + 1)

    def operator(c):
        zero = jnp.zeros((columns, columns), F32)
        return SHIFT * c + SCALE * jnp.concatenate((zero, c[: ITERS * columns]), axis=0)

    def inner(u, v):
        return dot(u.T, dot(hankel, v))

    shape = (hankel.shape[0], columns)
    same = lax.broadcasted_iota(jnp.int32, shape, 0) == lax.broadcasted_iota(jnp.int32, shape, 1)
    residual = jnp.where(same, 1.0, 0.0).astype(F32)
    direction, answer = residual, jnp.zeros(shape, F32)
    gamma = hankel[:columns, :columns]
    start = least_pivots(gamma)
    fine = jnp.ones((1, columns), F32)
    for iteration in range(ITERS):
        image = operator(direction)
        alpha = solve(inner(direction, image), gamma)
        answer = answer + dot(direction, alpha)
        if iteration + 1 < ITERS:
            residual = residual - dot(image, alpha)
            gamma_next = inner(residual, residual)
            fine = jnp.where(least_pivots(gamma_next) > FLOOR * start, fine, 0.0)
            beta = solve(gamma, gamma_next)
            direction = residual + dot(direction, beta)
            gamma = gamma_next
    return answer, fine


def final_kernel(c_ref, p0, p1, p2, x_ref, g_ref):
    quads, ys, both, depth, _ = p0.shape
    columns = quads * both
    tile = min(8, depth)
    basis = (p0, p1, p2)
    for half in range(2):
        span = range(half * columns // 2, (half + 1) * columns // 2)
        mix = [[c_ref[k * columns + i, p] for p in span] for k in range(3) for i in range(columns)]

        def body(step, carry):
            y = step // (depth // tile)
            rows = pl.ds(pl.multiple_of(step % (depth // tile) * tile, tile), tile)
            sums = [0.0] * len(span)
            for k in range(3):
                for i in range(columns):
                    value = basis[k][i // both, y, i % both, rows]
                    sums = [s + value * m for s, m in zip(sums, mix[k * columns + i])]
            grad = 0.0
            for s, p in zip(sums, span):
                x_ref[p // both, y, p % both, rows] = s
                if p == 0:
                    grad = grad + 0.5 * s * s
                else:
                    grad = grad - p0[p // both, y, p % both, rows] * s * (0.5 / (columns - 1))
            g_ref[y, rows] = grad if half == 0 else g_ref[y, rows] + grad
            return carry

        lax.fori_loop(0, ys * (depth // tile), body, 0)


MESH = pl.DeviceIdType.MESH


class Group:
    def __init__(self, sizes, axis):
        self.axis, self.size = axis, sizes[axis]
        self.names = tuple(sizes)
        self.place = {name: lax.axis_index(name) for name in sizes}
        self.me = self.place[axis]

    def peer(self, step):
        return lax.rem(self.me + step, self.size)

    def device(self, other):
        return tuple(other if name == self.axis else self.place[name] for name in self.names)

    def copy(self, src, dst, send, recv, other):
        return pltpu.make_async_remote_copy(
            src_ref=src, dst_ref=dst, send_sem=send, recv_sem=recv,
            device_id=self.device(other), device_id_type=MESH,
        )


def greet(groups):
    barrier = pltpu.get_barrier_semaphore()
    total = 0
    for group in groups:
        for step in range(1, group.size):
            pl.semaphore_signal(
                barrier, inc=1, device_id=group.device(group.peer(step)), device_id_type=MESH
            )
            total += 1
    pl.semaphore_wait(barrier, total)


def spread(group, source, target, send, recv):
    copies = []
    for step in range(1, group.size):
        copy = group.copy(
            source, target.at[group.me], send.at[step], recv.at[step], group.peer(step)
        )
        copy.start()
        copies.append(copy)
    target[group.me] = source[...]
    for copy in copies:
        copy.wait()
    total = target[0]
    for place in range(1, group.size):
        total = total + target[place]
    return total


def total_kernel(sizes, v_ref, o_ref, part, one, two, send, recv, send2, recv2):
    slab, pencil = Group(sizes, "slab"), Group(sizes, "pencil")
    greet((slab, pencil))
    part[...] = spread(pencil, v_ref, one, send, recv)
    o_ref[...] = spread(slab, part, two, send2, recv2)


def total_scratch(sizes, shape):
    return [
        pltpu.VMEM(shape, F32),
        pltpu.VMEM((sizes["pencil"],) + shape, F32),
        pltpu.VMEM((sizes["slab"],) + shape, F32),
        pltpu.SemaphoreType.DMA((sizes["pencil"],)),
        pltpu.SemaphoreType.DMA((sizes["pencil"],)),
        pltpu.SemaphoreType.DMA((sizes["slab"],)),
        pltpu.SemaphoreType.DMA((sizes["slab"],)),
    ]


def total_of(matrix):
    if INTERPRET:
        return lax.psum(matrix, ("slab", "pencil"))
    sizes = {name: lax.axis_size(name) for name in ("slab", "pencil")}
    rows, columns = matrix.shape
    wide = jnp.pad(matrix, ((0, 0), (0, 128 - columns)))
    found = pl.pallas_call(
        functools.partial(total_kernel, sizes),
        in_specs=[pl.BlockSpec(memory_space=pltpu.VMEM)],
        out_specs=pl.BlockSpec(memory_space=pltpu.VMEM),
        out_shape=jax.ShapeDtypeStruct(wide.shape, F32),
        scratch_shapes=total_scratch(sizes, wide.shape),
        compiler_params=pltpu.CompilerParams(collective_id=1, has_side_effects=True),
    )(wide)
    return found[:, :columns]


def krylov_kernel(
    sizes, plan,
    wf, field, spectrum, noise, seen, fx_h, fz_h, gx_h, gz_h, fy_h, gy_h,
    p1_o, p2_o, u2_o, c_ref, ok_ref,
    w0, wa, x1, x2, x3, eig, noi, see, put, got, tmp, p0, nown, sown,
    fx, fz, gx, gz, fy, gy, rows, stat, part_sum, one, two,
    xsend, xrecv, xown, zsend, zrecv, zown, hsend, hrecv, lsem, s1, r1, s2, r2,
):
    slab, pencil = Group(sizes, "slab"), Group(sizes, "pencil")
    slabs, pencils = slab.size, pencil.size
    _, ys, _, depth, nx = w0.shape
    part, wide = got[0].shape[1], got[0].shape[3]
    nz = wide // 2
    chunk, block, piece, odd = plan
    chunks, blocks = ys // chunk, part // block
    columns = field.shape[0] * 2
    tile = min(8, depth)
    depths = depth // tile

    tables = ((fx_h, fx), (fz_h, fz), (gx_h, gx), (gz_h, gz), (fy_h, fy), (gy_h, gy))
    loads = [pltpu.make_async_copy(a, b, lsem.at[i]) for i, (a, b) in enumerate(
        tables + ((field, p0), (noise, nown), (seen, sown)))]
    for load in loads:
        load.start()
    greet((slab, pencil))

    def zrows(ref, y, count):
        return ref.at[:, pl.ds(y, count)]

    def zcopies(number, slot, y, count, src, dst):
        made = []
        for step in range(1, slabs):
            other = slab.peer(step)
            made.append(slab.copy(
                src.at[other, pl.ds(y, count)], dst.at[slab.me, pl.ds(y, count)],
                zsend.at[number, slot, step], zrecv.at[number, slot, step], other,
            ))
        made.append(pltpu.make_async_copy(
            src.at[slab.me, pl.ds(y, count)], dst.at[slab.me, pl.ds(y, count)],
            zown.at[number, slot],
        ))
        return made

    def start(copies):
        for copy in copies:
            copy.start()

    def finish(copies):
        for copy in copies:
            copy.wait()

    gathers = ((spectrum, eig), (noise, noi), (seen, see))

    def hop(number, stage):
        own, full = gathers[number]
        sems = lambda way: (hsend.at[number, stage, way], hrecv.at[number, stage, way])

        def send(way, origin, other):
            src = own if stage == 0 else full.at[origin]
            slab.copy(src, full.at[origin], *sems(way), other).start()

        @pl.when((slab.me + 1 < slabs) & (slab.me >= stage))
        def _():
            send(0, slab.me - stage, slab.me + 1)

        @pl.when((slab.me >= 1) & (slab.me + stage < slabs))
        def _():
            send(1, slab.me + stage, slab.me - 1)

    def landed(number, stage):
        own, full = gathers[number]
        for way, origin, ok in (
            (0, slab.me - 1 - stage, slab.me >= 1 + stage),
            (1, slab.me + 1 + stage, slab.me + 1 + stage < slabs),
        ):
            @pl.when(ok)
            def _():
                slab.copy(
                    own, full.at[origin], hsend.at[number, stage, way],
                    hrecv.at[number, stage, way], slab.peer(1),
                ).wait_recv()

    def left(number, stage):
        own, full = gathers[number]
        for way, ok in (
            (0, (slab.me + 1 < slabs) & (slab.me >= stage)),
            (1, (slab.me >= 1) & (slab.me + stage < slabs)),
        ):
            @pl.when(ok)
            def _():
                slab.copy(
                    own, full.at[slab.me], hsend.at[number, stage, way],
                    hrecv.at[number, stage, way], slab.peer(1),
                ).wait_send()

    def xcopy(number, slot, step, view):
        other = pencil.peer(step)
        return pencil.copy(
            view(put[number % 2], other), view(got[number], pencil.me),
            xsend.at[number, slot, step], xrecv.at[number, slot, step], other,
        )

    def xself(number, slot, view):
        return pltpu.make_async_copy(
            view(put[number % 2], pencil.me), view(got[number], pencil.me), xown.at[number, slot]
        )

    def by_rows(c):
        return lambda ref, place: ref.at[place, :, pl.ds(c * chunk, chunk)]

    def by_part(b):
        return lambda ref, place: ref.at[place, pl.ds(b * block, block)]

    def xfinish(number, slots, view):
        for slot in range(slots):
            for step in range(1, pencils):
                xcopy(number, slot, step, view(slot)).wait()
            xself(number, slot, view(slot)).wait()

    def first_stage(j, real, imag):
        length = real.shape[1]
        data = split(jnp.concatenate((real, imag), axis=1))
        first = dot3((fx[0], fx[1]), data, ((1,), (1,)))
        first = jnp.concatenate((first[:length], first[length:]), axis=1)
        for q in range(pencils):
            tmp[j, q] = first[q * part : (q + 1) * part]

    def emit(number, c):
        span = pl.ds(c * chunk, chunk)

        def one_block(q):
            data = jnp.concatenate([tmp[j, q] for j in range(chunk)], axis=0)
            out = dot3(split(data), (fz[0], fz[1]))
            out = jnp.stack([out[j * part : (j + 1) * part] for j in range(chunk)])
            put[number % 2][q, :, span] = jnp.swapaxes(out, 0, 1)

        def body(step, carry):
            one_block(pencil.peer(step))
            xcopy(number, c, step, by_rows(c)).start()
            return carry

        lax.fori_loop(1, pencils, body, 0)
        one_block(pencil.me)
        xself(number, c, by_rows(c)).start()

    def absorb(number, c):
        span = pl.ds(c * chunk, chunk)

        def body(q, carry):
            data = jnp.swapaxes(got[number][q, :, span], 0, 1)
            data = jnp.concatenate([data[j] for j in range(chunk)], axis=0)
            out = dot3(split(data), (gz[0], gz[1]))
            for j in range(chunk):
                tmp[j, q] = out[j * part : (j + 1) * part]
            return carry

        lax.fori_loop(0, pencils, body, 0)

    def plane_back(j):
        first = jnp.concatenate([tmp[j, q] for q in range(pencils)], axis=0)
        first = jnp.concatenate((first[:, :nz], first[:, nz:]), axis=0)
        plane = dot3(split(first), (gx[0], gx[1]), ((0,), (0,)))
        return plane[:, :nx], plane[:, nx:]

    def lines(ref, y):
        return jnp.concatenate([ref[s, y] for s in range(slabs)], axis=0)

    def plane(ref, y, c):
        return jnp.concatenate([ref[s, y, c] for s in range(slabs)], axis=0)

    def store(ref, y, values):
        for c in range(2):
            for s in range(slabs):
                ref[s, y, c] = values[c][s * depth : (s + 1) * depth]

    def middle(number, after=None):
        def body(b, carry):
            for a2 in range(0, block, 2):
                spots = range(a2, min(a2 + 2, block))
                halves_of = []
                for a in spots:
                    data = jnp.concatenate(
                        [got[number][q, b * block + a] for q in range(pencils)], axis=0)
                    halves_of.append(jnp.concatenate((data[:, :nz], data[:, nz:]), axis=0))
                spec = dot3((fy[0], fy[1]), split(jnp.concatenate(halves_of, axis=1)))
                eigen = jnp.concatenate([
                    jnp.concatenate([eig[s, b * block + a] for s in range(slabs)], axis=0)
                    for a in spots], axis=1)
                spec = spec * jnp.concatenate((eigen, eigen), axis=0)
                back = dot3((gy[0], gy[1]), split(spec))
                ny = back.shape[0] // 2
                for k, a in enumerate(spots):
                    mine = back[:, k * nz : (k + 1) * nz]
                    mine = jnp.concatenate((mine[:ny], mine[ny:]), axis=1)
                    for q in range(pencils):
                        put[(number + 1) % 2][q, b * block + a] = mine[q * ys : (q + 1) * ys]
            for step in range(1, pencils):
                xcopy(number + 1, b, step, by_part(b)).start()
            xself(number + 1, b, by_part(b)).start()
            return carry

        lax.fori_loop(0, blocks, body, 0)

    def advance(number, old, new, target, which):
        for c in range(chunks):
            absorb(number, c)

            def body(j, carry):
                y = c * chunk + j
                found = plane_back(j)
                mask, shift = lines(see, y), lines(noi, y) - SHIFT
                values = tuple(
                    (mask * t + shift * plane(old, y, k)) * (1.0 / SCALE)
                    for k, t in enumerate(found)
                )
                store(new, y, values)
                first_stage(j, *values)
                return carry

            lax.fori_loop(0, chunk, body, 0)
            emit(number + 1, c)
            start(zcopies(which, c, c * chunk, chunk, new, target))

    pieces = ys // piece
    for k in range(pieces):
        start(zcopies(0, k, k * piece, piece, wf, w0))
    own_loads = [pltpu.make_async_copy(own, full.at[slab.me], lsem.at[len(loads) + i])
                 for i, (own, full) in enumerate(gathers)]
    start(own_loads)
    hop(0, 0)
    for load in loads[:6]:
        load.wait()
    for c in range(chunks):
        for k in range(c * chunk // piece, (c + 1) * chunk // piece):
            finish(zcopies(0, k, k * piece, piece, wf, w0))

            def enter(j, carry):
                y = k * piece + j
                first_stage(y - c * chunk, plane(w0, y, 0), plane(w0, y, 1))
                return carry

            lax.fori_loop(0, piece, enter, 0)
        emit(0, c)
    for stage in range(slabs - 1):
        landed(0, stage)
        if stage + 2 < slabs:
            hop(0, stage + 1)
        if stage == 0:
            hop(1, 0)
            hop(2, 0)
    finish(own_loads)
    xfinish(0, chunks, by_rows)
    middle(0)
    for stage in range(slabs - 1):
        for number in (1, 2):
            landed(number, stage)
            if stage + 2 < slabs:
                hop(number, stage + 1)
    xfinish(1, blocks, by_part)
    advance(1, w0, wa, x1, 1)
    xfinish(2, chunks, by_rows)
    middle(2)
    xfinish(3, blocks, by_part)
    advance(3, wa, w0, x2, 2)
    xfinish(4, chunks, by_rows)
    middle(4)
    for c in range(chunks):
        finish(zcopies(1, c, c * chunk, chunk, wa, x1))
    xfinish(5, blocks, by_part)
    for c in range(chunks):
        absorb(5, c)

        def leave(j, carry):
            store(wa, c * chunk + j, plane_back(j))
            return carry

        lax.fori_loop(0, chunk, leave, 0)
        start(zcopies(3, c, c * chunk, chunk, wa, x3))

    def spot(ref, i, y, z):
        return (ref, (i, y, 0, z) if odd else (i // 2, y, i % 2, z))

    def tiles(step, c):
        y = c * chunk + step // depths
        return y, pl.ds(pl.multiple_of(step % depths * tile, tile), tile)

    pairs = [(i, j) for i in range(columns) for j in range(i, columns)]
    zero = tuple(jnp.zeros((tile, nx), F32) for _ in pairs)
    lane = lax.broadcasted_iota(jnp.int32, stat.shape, 1)

    def at(ref, i, y, z):
        return ref[i, y, 0, z] if odd else ref[i // 2, y, i % 2, z]

    def base(ref, i, y, z):
        return ref[i // 2, y, i % 2, z]

    def note(moment, sums):
        for total, (i, j) in zip(sums, pairs):
            row = jnp.sum(total, axis=0, keepdims=True)
            rows[pl.ds(i * columns + j, 1)] = row
            if i != j:
                rows[pl.ds(j * columns + i, 1)] = row
        found = stat[...]
        for i in range(columns):
            column = jnp.sum(rows[pl.ds(i * columns, columns)], axis=1, keepdims=True)
            found = jnp.where(lane == moment * columns + i, column, found)
        stat[...] = found

    def moment(number, left_of, right_of):
        def body(step, sums):
            y, z = tiles(step, 0)
            lefts = [left_of(i, y, z) for i in range(columns)]
            rights = lefts if right_of is left_of else [right_of(i, y, z) for i in range(columns)]
            return tuple(s + lefts[i] * rights[j] for s, (i, j) in zip(sums, pairs))

        note(number, lax.fori_loop(0, ys * depths, body, zero))

    stat[...] = jnp.zeros(stat.shape, F32)
    for load in loads[6:]:
        load.wait()
    for c in range(chunks):
        finish(zcopies(2, c, c * chunk, chunk, w0, x2))

    def shape_basis(step, carry):
        y, z = tiles(step, 0)
        mask = sown[y, z] > 0
        factor = (nown[y, z] - SHIFT) * (1.0 / SCALE)
        for i in range(columns):
            once = factor * base(p0, i, y, z)
            place = (i, y, 0, z) if odd else (i // 2, y, i % 2, z)
            x1[place] = jnp.where(mask, x1[place], once)
            x2[place] = jnp.where(mask, x2[place], factor * once)
        return carry

    lax.fori_loop(0, ys * depths, shape_basis, 0)
    outs = [pltpu.make_async_copy(x1, p1_o, lsem.at[0]), pltpu.make_async_copy(x2, p2_o, lsem.at[1])]
    start(outs)
    of0, of1, of2 = (functools.partial(f, r) for f, r in ((base, p0), (at, x1), (at, x2)))
    for number, (l, r) in enumerate(((of0, of0), (of0, of1), (of1, of1), (of1, of2), (of2, of2))):
        moment(number, l, r)
    sums = zero
    for c in range(chunks):
        finish(zcopies(3, c, c * chunk, chunk, wa, x3))

        def last(step, sums):
            y, z = tiles(step, c)
            mask = sown[y, z] * (1.0 / SCALE)
            factor = (nown[y, z] - SHIFT) * (1.0 / SCALE)
            lefts, rights = [], []
            for i in range(columns):
                place = (i, y, 0, z) if odd else (i // 2, y, i % 2, z)
                lefts.append(x2[place])
                rights.append(mask * x3[place] + factor * lefts[-1])
                x3[place] = rights[-1]
            return tuple(s + lefts[i] * rights[j] for s, (i, j) in zip(sums, pairs))

        sums = lax.fori_loop(0, chunk * depths, last, sums)
    note(5, sums)
    out = pltpu.make_async_copy(x3, u2_o, lsem.at[2])
    out.start()
    for number in range(len(gathers)):
        for stage in range(slabs - 1):
            left(number, stage)
    part_sum[...] = spread(pencil, stat, one, s1, r1)
    found = spread(slab, part_sum, two, s2, r2)
    hankel = jnp.concatenate(
        [found[:, j * columns : (j + ITERS + 1) * columns] for j in range(ITERS + 1)], axis=0)
    c_ref[...], ok_ref[...] = small(hankel)
    finish(outs)
    out.wait()


def krylov(wf, field, spectrum, noise, seen, tables):
    sizes = {name: lax.axis_size(name) for name in ("slab", "pencil")}
    slabs, pencils = sizes["slab"], sizes["pencil"]
    quads, ys, _, depth, nx = field.shape
    columns = 2 * quads
    part, below, nz = spectrum.shape
    wide = 2 * nz
    chunk = 8 if ys % 8 == 0 else ys
    block = min(4, part)
    piece = min(4, chunk)
    planes = (slabs, ys, 2, depth, nx)
    gathered = (slabs, ys, depth, nx)
    sent = (pencils, part, ys, wide)
    slots = max(ys // chunk, part // block)
    any_space = pl.BlockSpec(memory_space=pl.ANY)
    vmem = pl.BlockSpec(memory_space=pltpu.VMEM)
    dma = pltpu.SemaphoreType.DMA
    tile = (columns, 128)
    scratch = (
        [pltpu.VMEM(planes, F32)] * 5
        + [pltpu.VMEM((slabs,) + spectrum.shape, F32)]
        + [pltpu.VMEM(gathered, F32)] * 2
        + [[pltpu.VMEM(sent, F32)] * 2, [pltpu.VMEM(sent, F32)] * 6]
        + [pltpu.VMEM((chunk, pencils, part, wide), F32), pltpu.VMEM(field.shape, F32)]
        + [pltpu.VMEM(noise.shape, F32)] * 2
        + [pltpu.VMEM(t.shape, BF16) for t in tables]
        + [pltpu.VMEM((columns * columns, nx), F32), pltpu.VMEM(tile, F32)]
        + total_scratch(sizes, tile)[:3]
        + [dma((6, slots, pencils))] * 2 + [dma((6, slots))]
        + [dma((4, ys // piece, slabs))] * 2 + [dma((4, ys // piece))]
        + [dma((3, slabs, 2))] * 2 + [dma((12,))]
        + total_scratch(sizes, tile)[3:]
    )
    return pl.pallas_call(
        functools.partial(krylov_kernel, sizes, (chunk, block, piece, slabs == columns)),
        in_specs=[any_space] * 11,
        out_specs=(any_space, any_space, any_space, vmem, vmem),
        out_shape=(jax.ShapeDtypeStruct(planes, F32),) * 3 + (
            jax.ShapeDtypeStruct(((ITERS + 1) * columns, columns), F32),
            jax.ShapeDtypeStruct((1, columns), F32),
        ),
        scratch_shapes=scratch,
        cost_estimate=pl.CostEstimate(flops=2**33, bytes_accessed=2**26, transcendentals=0),
        compiler_params=pltpu.CompilerParams(
            collective_id=0, has_side_effects=True, vmem_limit_bytes=60 * 2**20
        ),
    )(wf, field, spectrum, noise, seen, *tables)


def recurrences(p0, p1, p2, u2):
    flat = lambda v: jnp.swapaxes(v, 1, 2).reshape(v.shape[0] * v.shape[2], -1)
    basis = [flat(v) for v in (p0, p1, p2, u2)]
    columns = basis[0].shape[0]

    def field(c):
        return sum(dot(c[k].T, basis[k]) for k in range(len(c)))

    def gram(u, v):
        return total_of(jnp.dot(u, v.T, precision=precise))

    def operator(c):
        zero = jnp.zeros((1, columns, columns), F32)
        return SHIFT * jnp.concatenate((c, zero)) + SCALE * jnp.concatenate((zero, c))

    def longer(c):
        return jnp.concatenate((c, jnp.zeros((1, columns, columns), F32)))

    residual = direction = answer = jnp.eye(columns, dtype=F32)[None]
    answer = 0.0 * answer
    vector = field(residual)
    gamma = gram(vector, vector)
    for iteration in range(ITERS):
        image = operator(direction)
        alpha = solve(gram(field(direction), field(image)), gamma)
        answer = answer + jnp.einsum("kij,jp->kip", direction, alpha, precision=precise)
        if iteration + 1 < ITERS:
            residual = longer(residual) - jnp.einsum("kij,jp->kip", image, alpha, precision=precise)
            vector = field(residual)
            gamma_next = gram(vector, vector)
            beta = solve(gamma, gamma_next)
            direction = residual + longer(
                jnp.einsum("kij,jp->kip", direction, beta, precision=precise)
            )
            answer = longer(answer)
            gamma = gamma_next
    return answer.reshape(-1, columns)


def local(right_sides, spectrum, noise_var, observed):
    columns, depth, ys, nx = right_sides.shape
    slabs, pencils = lax.axis_size("slab"), lax.axis_size("pencil")
    nz, ny = depth * slabs, ys * pencils
    seen = jnp.swapaxes(observed.astype(F32), 0, 1)
    noise = jnp.swapaxes(noise_var, 0, 1)
    quads = columns // 2
    field = jnp.transpose(right_sides.reshape(quads, 2, depth, ys, nx), (0, 3, 1, 2, 4))
    odd = columns // slabs % 2

    fx, gx = halves(embed(nx, True)), halves(embed(nx, False).T)
    fz, gz = halves(embed(nz, True).T), halves(embed(nz, False).T)
    fy, gy = halves(embed(ny, True)), halves(embed(ny, False, 1.0 / (nx * ny * nz)))
    tables = [jnp.asarray(t) for t in (fx, fz, gx, gz, fy, gy)]

    masked = field * seen[None, :, None]
    if odd:
        masked = jnp.swapaxes(masked, 1, 2).reshape(columns, ys, 1, depth, nx)
        masked = jnp.concatenate((masked, jnp.zeros_like(masked)), axis=2)
    *basis, coefficients, fine = krylov(masked, field, spectrum, noise, seen, tables)
    if odd:
        basis = [
            jnp.swapaxes(v[:, :, 0].reshape(quads, 2, ys, depth, nx), 1, 2) for v in basis
        ]
    p1, p2, u2 = basis
    coefficients = lax.cond(
        jnp.min(fine) > 0.5,
        lambda: coefficients[: 3 * columns],
        lambda: recurrences(field, p1, p2, u2),
    )
    answer, grad = pl.pallas_call(
        final_kernel,
        in_specs=[pl.BlockSpec(memory_space=pltpu.SMEM)]
        + [pl.BlockSpec(memory_space=pltpu.VMEM)] * 3,
        out_shape=(
            jax.ShapeDtypeStruct(field.shape, F32),
            jax.ShapeDtypeStruct((ys, depth, nx), F32),
        ),
        interpret=INTERPRET,
    )(coefficients, field, p1, p2)
    answer = jnp.transpose(answer, (0, 2, 3, 1, 4)).reshape(columns, depth, ys, nx)
    return answer, jnp.swapaxes(grad, 0, 1)


def solution(mesh):
    in_specs = (
        P(None, "slab", "pencil", None),
        P("pencil", "slab", None),
        P("slab", "pencil", None),
        P("slab", "pencil", None),
    )
    out_specs = (P(None, "slab", "pencil", None), P("slab", "pencil", None))
    return jax.shard_map(local, mesh=mesh, in_specs=in_specs, out_specs=out_specs, check_vma=False)
```

time: 470 us -> 310 us (0.66)
  Pallas kernels: 430 us -> 294 us
  other arithmetic: 22.2 us -> 6 us
  local copies, waits for them, and re-layouts: 14.8 us -> 8.85 us
    pallas_call x24 -> x1, Pallas kernels: 417 us -> 281 us  [krylov(): pl.pallas_call(functools.partial(krylov_kernel, sizes, (chunk, block, pie...]
    reduce_sum x8 -> x0, other arithmetic: 7.26 us -> none  [the longest x6 5.17 us: moment(): return jnp.sum(rows, axis=1)]
    add x1 -> x0, other arithmetic: 6.83 us -> none  [local(): u2 = 1.0 / SCALE * seen_here * from_planes(t3) + factor * p2]
    slice x2 -> x0, local copies, waits for them, and re-layouts: 4.9 us -> none  [the longest x1 3.19 us: local(): got, high = travel(6, middle(got, eigen), (w2[:, ys // 2:], 'slab', False))]
where the time goes in v1:
time: 310 us
  Pallas kernels  294 us (95%)
  local copies, waits for them, and re-layouts  8.85 us (3%)
  other arithmetic  6 us (2%)
    pallas_call x1, Pallas kernels, krylov(): pl.pallas_call(functools.partial(krylov_kernel, sizes, (chunk, block, pie...  281 us
    pallas_call x1, Pallas kernels, local(): pl.pallas_call(final_kernel, in_specs=[pl.BlockSpec(memory_space=pltpu.SM...  12.3 us

profile of v1, /device:TPU:0, one launch (start us, length us, event | category | flops | bytes accessed | tf_op | source)
XLA Modules:
  0.0 310.0 jit_solution(18407463550211281720)
XLA Ops:
  0.6 1.0 fusion.51.seen
  1.7 0.0 copy-start.14
  1.7 1.8 copy.113
  3.5 0.0 copy-start.10
  3.5 3.7 %broadcast_multiply_fusion.wf = f32[4,16,2,32,128]{4,3,2,1,0:T(8,128)} fusion(f32[16,32,128]{2,1,0:T(8,128)S(1)} %fusion.51.seen, f32[4,2,32,16,128]{4,3,2,1,0:T(8,128)} %bitcast.290), kind=kLoop, calls=%fused_computation.235 | loop fusion | flops 524288 | bytes 4456448 | tf_op jit(solution)/shard_map/mul | solution.py:699
  7.2 0.0 copy-done.14
  7.2 0.0 copy-done.10
  7.3 2.0 copy.112
  9.2 281.4 %shard_map.113 = (f32[4,16,2,32,128]{4,3,2,1,0:T(8,128)}, f32[4,16,2,32,128]{4,3,2,1,0:T(8,128)}, f32[4,16,2,32,128]{4,3,2,1,0:T(8,128)}, f32[32,8]{1,0:T(8,128)S(1)}, f32[1,8]{1,0:T(1,128)}) custom-call(f32[4,16,2,32,128]{4,3,2,1,0:T(8,128)} %broadcast_multiply_fusion.wf, f32[4,16,2,32,128]{4,3,2,1,0:T(8,128)} %bitcast.293, f32[16,32,128]{2,1,0:T(8,128)} %spectrum.1, ...), custom_call_target="tpu_custom_call" | custom-call | flops 8589934592 | bytes 67108864 | tf_op jit(solution)/shard_map/pallas_call | solution.py:629
  290.6 1.2 reduce_min.9
  292.5 0.2 conditional.1
  292.8 12.3 %shard_map.114 = (f32[4,16,2,32,128]{4,3,2,1,0:T(8,128)}, f32[16,32,128]{2,1,0:T(8,128)}) custom-call(f32[24,8]{1,0:T(8,128)S(1)} %get-tuple-element.46.c_ref, f32[4,16,2,32,128]{4,3,2,1,0:T(8,128)} %bitcast.294, f32[4,16,2,32,128]{4,3,2,1,0:T(8,128)} %get-tuple-element.26.p1, f32[4,16,2,32,128]{4,3,2,1,0:T(8,128)} %get-tuple-element.27.p2), custom_call_target="tpu_custom_call" | custom-call | tf_op jit(solution)/shard_map/pallas_call | solution.py:714
  305.0 0.0 copy-start.15
  305.0 4.1 %copy.93 = f32[4,2,32,16,128]{4,3,2,1,0:T(8,128)} copy(f32[4,2,32,16,128]{4,2,1,3,0:T(8,128)} %bitcast.298) | data formatting | bytes 4194304 | tf_op jit(solution)/shard_map/transpose | solution.py:724
  309.2 0.0 copy-done.15
  309.2 0.9 copy.94
  (1 shorter events, 0.0 us)
Async XLA Ops:
  1.7 5.6 %copy-start.14 = (f32[16,32,128]{2,1,0:T(8,128)}, f32[16,32,128]{2,1,0:T(8,128)S(1)}, u32[]{:S(2)}) copy-start(f32[16,32,128]{2,1,0:T(8,128)S(1)} %fusion.51.seen) | copy-start | bytes 786436
  3.5 3.7 %copy-start.10 = (f32[8,32,16,128]{3,2,1,0:T(8,128)S(1)}, f32[8,32,16,128]{3,2,1,0:T(8,128)}, u32[]{:S(2)}) copy-start(f32[8,32,16,128]{3,2,1,0:T(8,128)} %param.12) | copy-start | bytes 6291460
  305.0 4.2 %copy-start.15 = (f32[16,32,128]{2,1,0:T(8,128)S(1)}, f32[16,32,128]{2,1,0:T(8,128)}, u32[]{:S(2)}) copy-start(f32[16,32,128]{2,1,0:T(8,128)} %get-tuple-element.31) | copy-start | bytes 786436

commit v2 on v1

--- a/solution.py
+++ b/solution.py
@@ -103,36 +103,35 @@
     return answer, fine
 
 
-def final_kernel(c_ref, p0, p1, p2, x_ref, g_ref):
-    quads, ys, both, depth, _ = p0.shape
-    columns = quads * both
-    tile = min(8, depth)
-    basis = (p0, p1, p2)
-    for half in range(2):
-        span = range(half * columns // 2, (half + 1) * columns // 2)
-        mix = [[c_ref[k * columns + i, p] for p in span] for k in range(3) for i in range(columns)]
-
-        def body(step, carry):
-            y = step // (depth // tile)
-            rows = pl.ds(pl.multiple_of(step % (depth // tile) * tile, tile), tile)
-            sums = [0.0] * len(span)
-            for k in range(3):
+def final_kernel(odd, c_ref, right, p1, p2, x_ref, g_ref):
+    columns, tile, ys, _ = right.shape
+    chunk = 8 if ys % 8 == 0 else ys
+
+    def at(ref, i, y):
+        return ref[i, pl.ds(y, chunk), 0] if odd else ref[i // 2, pl.ds(y, chunk), i % 2]
+
+    for y in range(0, ys, chunk):
+        rows = pl.ds(y, chunk)
+
+        def column(p):
+            found = 0.0
+            for k, ref in ((1, p1), (2, p2)):
                 for i in range(columns):
-                    value = basis[k][i // both, y, i % both, rows]
-                    sums = [s + value * m for s, m in zip(sums, mix[k * columns + i])]
-            grad = 0.0
-            for s, p in zip(sums, span):
-                x_ref[p // both, y, p % both, rows] = s
-                if p == 0:
-                    grad = grad + 0.5 * s * s
-                else:
-                    grad = grad - p0[p // both, y, p % both, rows] * s * (0.5 / (columns - 1))
-            g_ref[y, rows] = grad if half == 0 else g_ref[y, rows] + grad
-            return carry
-
-        lax.fori_loop(0, ys * (depth // tile), body, 0)
-
-
+                    found = found + at(ref, i, y) * c_ref[k * columns + i, p]
+            found = jnp.swapaxes(found, 0, 1)
+            for i in range(columns):
+                found = found + right[i, :, rows] * c_ref[i, p]
+            x_ref[p, :, rows] = found
+            return found
+
+        def body(p, grad):
+            return grad - right[p, :, rows] * column(p) * (0.5 / (columns - 1))
+
+        first = column(0)
+        g_ref[:, rows] = lax.fori_loop(1, columns, body, 0.5 * first * first)
+
+
+QU, YU = 4, 4
 MESH = pl.DeviceIdType.MESH
 
 
@@ -223,9 +222,9 @@
 
 def krylov_kernel(
     sizes, plan,
-    wf, field, spectrum, noise, seen, fx_h, fz_h, gx_h, gz_h, fy_h, gy_h,
+    right, spectrum, noise, seen, fx_h, fz_h, gx_h, gz_h, fy_h, gy_h,
     p1_o, p2_o, u2_o, c_ref, ok_ref,
-    w0, wa, x1, x2, x3, eig, noi, see, put, got, tmp, p0, nown, sown,
+    w0, wa, x1, x2, x3, eig, noi, see, put, got, tmp, p0, nown, sown, nat, nnat, snat,
     fx, fz, gx, gz, fy, gy, rows, stat, part_sum, one, two,
     xsend, xrecv, xown, zsend, zrecv, zown, hsend, hrecv, lsem, s1, r1, s2, r2,
 ):
@@ -234,15 +233,27 @@
     _, ys, _, depth, nx = w0.shape
     part, wide = got[0].shape[1], got[0].shape[3]
     nz = wide // 2
-    chunk, block, piece, odd = plan
+    chunk, block, piece, odd, enter_groups, groups = plan
     chunks, blocks = ys // chunk, part // block
-    columns = field.shape[0] * 2
+    columns = right.shape[0]
     tile = min(8, depth)
     depths = depth // tile
 
+    def brought(slot, src, dst):
+        return pltpu.make_async_copy(src, dst, lsem.at[slot])
+
+    naturals = []
+    for c in range(chunks):
+        span = pl.ds(c * chunk, chunk)
+        naturals.append([
+            brought(4 * c, seen.at[:, span], snat.at[:, span]),
+            brought(4 * c + 1, right.at[:, :, span], nat.at[:, :, span]),
+            brought(4 * c + 2, noise.at[:, span], nnat.at[:, span]),
+        ])
+        for load in naturals[-1]:
+            load.start()
     tables = ((fx_h, fx), (fz_h, fz), (gx_h, gx), (gz_h, gz), (fy_h, fy), (gy_h, gy))
-    loads = [pltpu.make_async_copy(a, b, lsem.at[i]) for i, (a, b) in enumerate(
-        tables + ((field, p0), (noise, nown), (seen, sown)))]
+    loads = [brought(4 * chunks + i, a, b) for i, (a, b) in enumerate(tables)]
     for load in loads:
         load.start()
     greet((slab, pencil))
@@ -272,15 +283,23 @@
         for copy in copies:
             copy.wait()
 
-    gathers = ((spectrum, eig), (noise, noi), (seen, see))
+    gathers = [(spectrum, lambda place: eig.at[place])]
+    for c in range(chunks):
+        span = pl.ds(c * chunk, chunk)
+        for own, full in ((nown, noi), (sown, see)):
+            gathers.append((
+                own.at[span],
+                functools.partial(lambda full, span, place: full.at[place, span], full, span),
+            ))
+    stages = [0] * len(gathers)
 
     def hop(number, stage):
         own, full = gathers[number]
         sems = lambda way: (hsend.at[number, stage, way], hrecv.at[number, stage, way])
 
         def send(way, origin, other):
-            src = own if stage == 0 else full.at[origin]
-            slab.copy(src, full.at[origin], *sems(way), other).start()
+            src = own if stage == 0 else full(origin)
+            slab.copy(src, full(origin), *sems(way), other).start()
 
         @pl.when((slab.me + 1 < slabs) & (slab.me >= stage))
         def _():
@@ -290,31 +309,46 @@
         def _():
             send(1, slab.me + stage, slab.me - 1)
 
+    def halted(number, stage, way):
+        own, full = gathers[number]
+        return slab.copy(
+            own, full(slab.me), hsend.at[number, stage, way], hrecv.at[number, stage, way],
+            slab.peer(1),
+        )
+
     def landed(number, stage):
-        own, full = gathers[number]
-        for way, origin, ok in (
-            (0, slab.me - 1 - stage, slab.me >= 1 + stage),
-            (1, slab.me + 1 + stage, slab.me + 1 + stage < slabs),
-        ):
-            @pl.when(ok)
-            def _():
-                slab.copy(
-                    own, full.at[origin], hsend.at[number, stage, way],
-                    hrecv.at[number, stage, way], slab.peer(1),
-                ).wait_recv()
+        @pl.when(slab.me >= 1 + stage)
+        def _():
+            halted(number, stage, 0).wait_recv()
+
+        @pl.when(slab.me + 1 + stage < slabs)
+        def _():
+            halted(number, stage, 1).wait_recv()
 
     def left(number, stage):
-        own, full = gathers[number]
-        for way, ok in (
-            (0, (slab.me + 1 < slabs) & (slab.me >= stage)),
-            (1, (slab.me >= 1) & (slab.me + stage < slabs)),
-        ):
-            @pl.when(ok)
-            def _():
-                slab.copy(
-                    own, full.at[slab.me], hsend.at[number, stage, way],
-                    hrecv.at[number, stage, way], slab.peer(1),
-                ).wait_send()
+        @pl.when((slab.me + 1 < slabs) & (slab.me >= stage))
+        def _():
+            halted(number, stage, 0).wait_send()
+
+        @pl.when((slab.me >= 1) & (slab.me + stage < slabs))
+        def _():
+            halted(number, stage, 1).wait_send()
+
+    def relay(*numbers):
+        for number in numbers:
+            stage = stages[number]
+            if stage + 1 < slabs:
+                landed(number, stage)
+                if stage + 2 < slabs:
+                    hop(number, stage + 1)
+                stages[number] = stage + 1
+
+    def complete(*numbers):
+        for _ in range(slabs - 1):
+            relay(*numbers)
+
+    def of_rows(c):
+        return (1 + 2 * c, 2 + 2 * c)
 
     def xcopy(number, slot, step, view):
         other = pencil.peer(step)
@@ -328,17 +362,17 @@
             view(put[number % 2], pencil.me), view(got[number], pencil.me), xown.at[number, slot]
         )
 
-    def by_rows(c):
-        return lambda ref, place: ref.at[place, :, pl.ds(c * chunk, chunk)]
+    def by_rows(group):
+        return lambda ref, place: ref.at[place, :, pl.ds(*group)]
 
     def by_part(b):
         return lambda ref, place: ref.at[place, pl.ds(b * block, block)]
 
-    def xfinish(number, slots, view):
-        for slot in range(slots):
+    def xfinish(number, views):
+        for slot, view in enumerate(views):
             for step in range(1, pencils):
-                xcopy(number, slot, step, view(slot)).wait()
-            xself(number, slot, view(slot)).wait()
+                xcopy(number, slot, step, view).wait()
+            xself(number, slot, view).wait()
 
     def first_stage(j, real, imag):
         length = real.shape[1]
@@ -348,36 +382,36 @@
         for q in range(pencils):
             tmp[j, q] = first[q * part : (q + 1) * part]
 
-    def emit(number, c):
-        span = pl.ds(c * chunk, chunk)
+    def emit(number, slot, group):
+        span, count = pl.ds(*group), group[1]
 
         def one_block(q):
-            data = jnp.concatenate([tmp[j, q] for j in range(chunk)], axis=0)
+            data = jnp.concatenate([tmp[j, q] for j in range(count)], axis=0)
             out = dot3(split(data), (fz[0], fz[1]))
-            out = jnp.stack([out[j * part : (j + 1) * part] for j in range(chunk)])
+            out = jnp.stack([out[j * part : (j + 1) * part] for j in range(count)])
             put[number % 2][q, :, span] = jnp.swapaxes(out, 0, 1)
 
         def body(step, carry):
             one_block(pencil.peer(step))
-            xcopy(number, c, step, by_rows(c)).start()
+            xcopy(number, slot, step, by_rows(group)).start()
             return carry
 
-        lax.fori_loop(1, pencils, body, 0)
+        lax.fori_loop(1, pencils, body, 0, unroll=QU)
         one_block(pencil.me)
-        xself(number, c, by_rows(c)).start()
-
-    def absorb(number, c):
-        span = pl.ds(c * chunk, chunk)
+        xself(number, slot, by_rows(group)).start()
+
+    def absorb(number, group):
+        span, count = pl.ds(*group), group[1]
 
         def body(q, carry):
             data = jnp.swapaxes(got[number][q, :, span], 0, 1)
-            data = jnp.concatenate([data[j] for j in range(chunk)], axis=0)
+            data = jnp.concatenate([data[j] for j in range(count)], axis=0)
             out = dot3(split(data), (gz[0], gz[1]))
-            for j in range(chunk):
+            for j in range(count):
                 tmp[j, q] = out[j * part : (j + 1) * part]
             return carry
 
-        lax.fori_loop(0, pencils, body, 0)
+        lax.fori_loop(0, pencils, body, 0, unroll=QU)
 
     def plane_back(j):
         first = jnp.concatenate([tmp[j, q] for q in range(pencils)], axis=0)
@@ -424,12 +458,15 @@
 
         lax.fori_loop(0, blocks, body, 0)
 
-    def advance(number, old, new, target, which):
-        for c in range(chunks):
-            absorb(number, c)
+    def advance(number, old, new, target, which, ready=None):
+        for slot, group in enumerate(groups):
+            start_row, count = group
+            absorb(number, group)
+            if ready is not None:
+                ready(start_row // chunk)
 
             def body(j, carry):
-                y = c * chunk + j
+                y = start_row + j
                 found = plane_back(j)
                 mask, shift = lines(see, y), lines(noi, y) - SHIFT
                 values = tuple(
@@ -440,71 +477,100 @@
                 first_stage(j, *values)
                 return carry
 
-            lax.fori_loop(0, chunk, body, 0)
-            emit(number + 1, c)
-            start(zcopies(which, c, c * chunk, chunk, new, target))
+            lax.fori_loop(0, count, body, 0, unroll=YU)
+            emit(number + 1, slot, group)
+            start(zcopies(which, slot, *group, new, target))
+
+    def turn(c):
+        for load in naturals[c]:
+            load.wait()
+        rows_of = pl.ds(c * chunk, chunk)
+
+        def body(k, carry):
+            deep = pl.ds(pl.multiple_of(k * tile, tile), tile)
+            mask = jnp.swapaxes(snat[deep, rows_of], 0, 1).astype(F32)
+            sown[rows_of, deep] = mask
+            nown[rows_of, deep] = jnp.swapaxes(nnat[deep, rows_of], 0, 1)
+            for i in range(columns):
+                values = jnp.swapaxes(nat[i, deep, rows_of], 0, 1)
+                p0[i // 2, rows_of, i % 2, deep] = values
+                if odd:
+                    wa[i, rows_of, 0, deep] = values * mask
+                    wa[i, rows_of, 1, deep] = jnp.zeros_like(values)
+                else:
+                    wa[i // 2, rows_of, i % 2, deep] = values * mask
+            return carry
+
+        lax.fori_loop(0, depths, body, 0)
 
     pieces = ys // piece
-    for k in range(pieces):
-        start(zcopies(0, k, k * piece, piece, wf, w0))
-    own_loads = [pltpu.make_async_copy(own, full.at[slab.me], lsem.at[len(loads) + i])
-                 for i, (own, full) in enumerate(gathers)]
+    early = max(pieces - 1, 1)
+    hop(0, 0)
+    for c in range(chunks):
+        turn(c)
+        for k in range(c * chunk // piece, (c + 1) * chunk // piece):
+            if k < early:
+                start(zcopies(0, k, k * piece, piece, wa, w0))
+    own_loads = [
+        brought(0, spectrum, eig.at[slab.me]), brought(1, nown, noi.at[slab.me]),
+        brought(2, sown, see.at[slab.me]),
+    ]
     start(own_loads)
-    hop(0, 0)
-    for load in loads[:6]:
+    relay(0)
+    for k in range(early, pieces):
+        start(zcopies(0, k, k * piece, piece, wa, w0))
+    for load in loads:
         load.wait()
-    for c in range(chunks):
-        for k in range(c * chunk // piece, (c + 1) * chunk // piece):
-            finish(zcopies(0, k, k * piece, piece, wf, w0))
+    for slot, (row, count) in enumerate(enter_groups):
+        for k in range(row // piece, (row + count) // piece):
+            finish(zcopies(0, k, k * piece, piece, wa, w0))
 
             def enter(j, carry):
                 y = k * piece + j
-                first_stage(y - c * chunk, plane(w0, y, 0), plane(w0, y, 1))
+                first_stage(y - row, plane(w0, y, 0), plane(w0, y, 1))
                 return carry
 
-            lax.fori_loop(0, piece, enter, 0)
-        emit(0, c)
-    for stage in range(slabs - 1):
-        landed(0, stage)
-        if stage + 2 < slabs:
-            hop(0, stage + 1)
-        if stage == 0:
-            hop(1, 0)
-            hop(2, 0)
+            lax.fori_loop(0, piece, enter, 0, unroll=YU)
+        if slot == max(len(enter_groups) - 2, 0):
+            relay(0)
+            for number in of_rows(0):
+                hop(number, 0)
+        emit(0, slot, (row, count))
+    complete(0)
+    relay(*of_rows(0))
+    for c in range(1, chunks):
+        for number in of_rows(c):
+            hop(number, 0)
     finish(own_loads)
-    xfinish(0, chunks, by_rows)
+    xfinish(0, [by_rows(group) for group in enter_groups])
     middle(0)
-    for stage in range(slabs - 1):
-        for number in (1, 2):
-            landed(number, stage)
-            if stage + 2 < slabs:
-                hop(number, stage + 1)
-    xfinish(1, blocks, by_part)
-    advance(1, w0, wa, x1, 1)
-    xfinish(2, chunks, by_rows)
+    for c in range(chunks):
+        relay(*of_rows(c))
+    for c in range(1, chunks):
+        relay(*of_rows(c))
+    xfinish(1, [by_part(b) for b in range(blocks)])
+    advance(1, w0, wa, x1, 1, lambda c: complete(*of_rows(c)))
+    xfinish(2, [by_rows(group) for group in groups])
     middle(2)
-    xfinish(3, blocks, by_part)
+    xfinish(3, [by_part(b) for b in range(blocks)])
     advance(3, wa, w0, x2, 2)
-    xfinish(4, chunks, by_rows)
+    xfinish(4, [by_rows(group) for group in groups])
     middle(4)
-    for c in range(chunks):
-        finish(zcopies(1, c, c * chunk, chunk, wa, x1))
-    xfinish(5, blocks, by_part)
-    for c in range(chunks):
-        absorb(5, c)
+    for slot, group in enumerate(groups):
+        finish(zcopies(1, slot, *group, wa, x1))
+    xfinish(5, [by_part(b) for b in range(blocks)])
+    for slot, group in enumerate(groups):
+        absorb(5, group)
 
         def leave(j, carry):
-            store(wa, c * chunk + j, plane_back(j))
+            store(wa, group[0] + j, plane_back(j))
             return carry
 
-        lax.fori_loop(0, chunk, leave, 0)
-        start(zcopies(3, c, c * chunk, chunk, wa, x3))
-
-    def spot(ref, i, y, z):
-        return (ref, (i, y, 0, z) if odd else (i // 2, y, i % 2, z))
-
-    def tiles(step, c):
-        y = c * chunk + step // depths
+        lax.fori_loop(0, group[1], leave, 0, unroll=YU)
+        start(zcopies(3, slot, *group, wa, x3))
+
+    def tiles(step, row):
+        y = row + step // depths
         return y, pl.ds(pl.multiple_of(step % depths * tile, tile), tile)
 
     pairs = [(i, j) for i in range(columns) for j in range(i, columns)]
@@ -539,10 +605,8 @@
         note(number, lax.fori_loop(0, ys * depths, body, zero))
 
     stat[...] = jnp.zeros(stat.shape, F32)
-    for load in loads[6:]:
-        load.wait()
-    for c in range(chunks):
-        finish(zcopies(2, c, c * chunk, chunk, w0, x2))
+    for slot, group in enumerate(groups):
+        finish(zcopies(2, slot, *group, w0, x2))
 
     def shape_basis(step, carry):
         y, z = tiles(step, 0)
@@ -562,11 +626,11 @@
     for number, (l, r) in enumerate(((of0, of0), (of0, of1), (of1, of1), (of1, of2), (of2, of2))):
         moment(number, l, r)
     sums = zero
-    for c in range(chunks):
-        finish(zcopies(3, c, c * chunk, chunk, wa, x3))
+    for slot, group in enumerate(groups):
+        finish(zcopies(3, slot, *group, wa, x3))
 
         def last(step, sums):
-            y, z = tiles(step, c)
+            y, z = tiles(step, group[0])
             mask = sown[y, z] * (1.0 / SCALE)
             factor = (nown[y, z] - SHIFT) * (1.0 / SCALE)
             lefts, rights = [], []
@@ -577,7 +641,7 @@
                 x3[place] = rights[-1]
             return tuple(s + lefts[i] * rights[j] for s, (i, j) in zip(sums, pairs))
 
-        sums = lax.fori_loop(0, chunk * depths, last, sums)
+        sums = lax.fori_loop(0, group[1] * depths, last, sums)
     note(5, sums)
     out = pltpu.make_async_copy(x3, u2_o, lsem.at[2])
     out.start()
@@ -593,11 +657,11 @@
     out.wait()
 
 
-def krylov(wf, field, spectrum, noise, seen, tables):
+def krylov(right, spectrum, noise, seen, tables):
     sizes = {name: lax.axis_size(name) for name in ("slab", "pencil")}
     slabs, pencils = sizes["slab"], sizes["pencil"]
-    quads, ys, _, depth, nx = field.shape
-    columns = 2 * quads
+    columns, depth, ys, nx = right.shape
+    quads = columns // 2
     part, below, nz = spectrum.shape
     wide = 2 * nz
     chunk = 8 if ys % 8 == 0 else ys
@@ -606,7 +670,12 @@
     planes = (slabs, ys, 2, depth, nx)
     gathered = (slabs, ys, depth, nx)
     sent = (pencils, part, ys, wide)
-    slots = max(ys // chunk, part // block)
+    groups = [(row, chunk) for row in range(0, ys, chunk)]
+    enter_groups = groups[:-1] + [
+        (row, piece) for row in range(groups[-1][0], ys, piece)
+    ]
+    slots = max(len(enter_groups), len(groups), part // block)
+    chunks = ys // chunk
     any_space = pl.BlockSpec(memory_space=pl.ANY)
     vmem = pl.BlockSpec(memory_space=pltpu.VMEM)
     dma = pltpu.SemaphoreType.DMA
@@ -616,19 +685,22 @@
         + [pltpu.VMEM((slabs,) + spectrum.shape, F32)]
         + [pltpu.VMEM(gathered, F32)] * 2
         + [[pltpu.VMEM(sent, F32)] * 2, [pltpu.VMEM(sent, F32)] * 6]
-        + [pltpu.VMEM((chunk, pencils, part, wide), F32), pltpu.VMEM(field.shape, F32)]
-        + [pltpu.VMEM(noise.shape, F32)] * 2
+        + [pltpu.VMEM((chunk, pencils, part, wide), F32)]
+        + [pltpu.VMEM((quads, ys, 2, depth, nx), F32)]
+        + [pltpu.VMEM((ys, depth, nx), F32)] * 2
+        + [pltpu.VMEM(v.shape, v.dtype) for v in (right, noise, seen)]
         + [pltpu.VMEM(t.shape, BF16) for t in tables]
         + [pltpu.VMEM((columns * columns, nx), F32), pltpu.VMEM(tile, F32)]
         + total_scratch(sizes, tile)[:3]
         + [dma((6, slots, pencils))] * 2 + [dma((6, slots))]
         + [dma((4, ys // piece, slabs))] * 2 + [dma((4, ys // piece))]
-        + [dma((3, slabs, 2))] * 2 + [dma((12,))]
+        + [dma((1 + 2 * chunks, slabs, 2))] * 2 + [dma((4 * chunks + 6,))]
         + total_scratch(sizes, tile)[3:]
     )
     return pl.pallas_call(
-        functools.partial(krylov_kernel, sizes, (chunk, block, piece, slabs == columns)),
-        in_specs=[any_space] * 11,
+        functools.partial(krylov_kernel, sizes, (
+            chunk, block, piece, slabs == columns, enter_groups, groups)),
+        in_specs=[any_space] * 10,
         out_specs=(any_space, any_space, any_space, vmem, vmem),
         out_shape=(jax.ShapeDtypeStruct(planes, F32),) * 3 + (
             jax.ShapeDtypeStruct(((ITERS + 1) * columns, columns), F32),
@@ -639,7 +711,7 @@
         compiler_params=pltpu.CompilerParams(
             collective_id=0, has_side_effects=True, vmem_limit_bytes=60 * 2**20
         ),
-    )(wf, field, spectrum, noise, seen, *tables)
+    )(right, spectrum, noise, seen, *tables)
 
 
 def recurrences(p0, p1, p2, u2):
@@ -685,44 +757,40 @@
     columns, depth, ys, nx = right_sides.shape
     slabs, pencils = lax.axis_size("slab"), lax.axis_size("pencil")
     nz, ny = depth * slabs, ys * pencils
-    seen = jnp.swapaxes(observed.astype(F32), 0, 1)
-    noise = jnp.swapaxes(noise_var, 0, 1)
     quads = columns // 2
-    field = jnp.transpose(right_sides.reshape(quads, 2, depth, ys, nx), (0, 3, 1, 2, 4))
-    odd = columns // slabs % 2
+    odd = slabs == columns
 
     fx, gx = halves(embed(nx, True)), halves(embed(nx, False).T)
     fz, gz = halves(embed(nz, True).T), halves(embed(nz, False).T)
     fy, gy = halves(embed(ny, True)), halves(embed(ny, False, 1.0 / (nx * ny * nz)))
     tables = [jnp.asarray(t) for t in (fx, fz, gx, gz, fy, gy)]
-
-    masked = field * seen[None, :, None]
-    if odd:
-        masked = jnp.swapaxes(masked, 1, 2).reshape(columns, ys, 1, depth, nx)
-        masked = jnp.concatenate((masked, jnp.zeros_like(masked)), axis=2)
-    *basis, coefficients, fine = krylov(masked, field, spectrum, noise, seen, tables)
-    if odd:
-        basis = [
-            jnp.swapaxes(v[:, :, 0].reshape(quads, 2, ys, depth, nx), 1, 2) for v in basis
-        ]
-    p1, p2, u2 = basis
+    p1, p2, u2, coefficients, fine = krylov(right_sides, spectrum, noise_var, observed, tables)
+
+    def slow():
+        field = jnp.transpose(right_sides.reshape(quads, 2, depth, ys, nx), (0, 3, 1, 2, 4))
+        basis = (p1, p2, u2)
+        if odd:
+            basis = [
+                jnp.swapaxes(v[:, :, 0].reshape(quads, 2, ys, depth, nx), 1, 2) for v in basis
+            ]
+        return recurrences(field, *basis)
+
     coefficients = lax.cond(
-        jnp.min(fine) > 0.5,
-        lambda: coefficients[: 3 * columns],
-        lambda: recurrences(field, p1, p2, u2),
+        jnp.min(fine) > 0.5, lambda: coefficients[: 3 * columns], slow
     )
-    answer, grad = pl.pallas_call(
-        final_kernel,
-        in_specs=[pl.BlockSpec(memory_space=pltpu.SMEM)]
-        + [pl.BlockSpec(memory_space=pltpu.VMEM)] * 3,
+    tile = min(8, depth)
+    planes = pl.BlockSpec(p1.shape[:3] + (tile, nx), lambda i: (0, 0, 0, i, 0))
+    natural = pl.BlockSpec((columns, tile, ys, nx), lambda i: (0, i, 0, 0))
+    return tuple(pl.pallas_call(
+        functools.partial(final_kernel, odd),
+        grid=(depth // tile,),
+        in_specs=[pl.BlockSpec(memory_space=pltpu.SMEM), natural, planes, planes],
+        out_specs=(natural, pl.BlockSpec((tile, ys, nx), lambda i: (i, 0, 0))),
         out_shape=(
-            jax.ShapeDtypeStruct(field.shape, F32),
-            jax.ShapeDtypeStruct((ys, depth, nx), F32),
+            jax.ShapeDtypeStruct(right_sides.shape, F32),
+            jax.ShapeDtypeStruct((depth, ys, nx), F32),
         ),
-        interpret=INTERPRET,
-    )(coefficients, field, p1, p2)
-    answer = jnp.transpose(answer, (0, 2, 3, 1, 4)).reshape(columns, depth, ys, nx)
-    return answer, jnp.swapaxes(grad, 0, 1)
+    )(coefficients, right_sides, p1, p2))
 
 
 def solution(mesh):

time: 310 us -> 282 us (0.910)
  Pallas kernels: 294 us -> 279 us
  local copies, waits for them, and re-layouts: 8.85 us -> 0.01 us
  other arithmetic: 6 us -> 1.22 us
    pallas_call x1, Pallas kernels: 281 us -> 271 us  [krylov(): pl.pallas_call(functools.partial(krylov_kernel, sizes, (chunk, block, pie...]
    pallas_call x1, Pallas kernels: 12.3 us -> 7.46 us  [local(): pl.pallas_call(functools.partial(final_kernel, odd), grid=(depth // tile,...]
    transpose x1 -> x0, local copies, waits for them, and re-layouts: 4.15 us -> none  [local(): jnp.transpose(answer, (0, 2, 3, 1, 4)).reshape(columns, depth, ys, nx)]
    mul x1 -> x0, other arithmetic: 3.73 us -> none  [local(): masked = field * seen[None, :, None]]
where the time goes in v2:
time: 282 us
  Pallas kernels  279 us (99%)
    pallas_call x1, Pallas kernels, krylov(): pl.pallas_call(functools.partial(krylov_kernel, sizes, (chunk, block, pie...  271 us
    pallas_call x1, Pallas kernels, local(): pl.pallas_call(functools.partial(final_kernel, odd), grid=(depth // tile,...  7.46 us

profile of v2, /device:TPU:0, one launch (start us, length us, event | category | flops | bytes accessed | tf_op | source)
XLA Modules:
  0.0 281.5 jit_solution(4119221253777321766)
XLA Ops:
  0.6 0.0 copy-start.10
  0.6 271.3 %shard_map.113 = (f32[4,16,2,32,128]{4,3,2,1,0:T(8,128)}, f32[4,16,2,32,128]{4,3,2,1,0:T(8,128)}, f32[4,16,2,32,128]{4,3,2,1,0:T(8,128)}, f32[32,8]{1,0:T(8,128)S(1)}, f32[1,8]{1,0:T(1,128)}) custom-call(f32[8,32,16,128]{3,2,1,0:T(8,128)} %right.3, f32[16,32,128]{2,1,0:T(8,128)} %spectrum.1, f32[32,16,128]{2,1,0:T(8,128)} %noise.1, s32[32,16,128]{2,1,0:T(8,128)} %seen.1, ...), custom_call_target="tpu_custom_call" | custom-call | flops 8589934592 | bytes 67108864 | tf_op jit(solution)/shard_map/pallas_call | solution.py:700
  271.9 1.2 reduce_min.9
  273.8 0.0 copy-done.10
  273.8 0.3 conditional.1
  274.1 7.5 %shard_map.114 = (f32[8,32,16,128]{3,2,1,0:T(8,128)}, f32[32,16,128]{2,1,0:T(8,128)}) custom-call(f32[24,8]{1,0:T(8,128)S(1)} %get-tuple-element.34.c_ref, f32[8,32,16,128]{3,2,1,0:T(8,128)} %right.3, f32[4,16,2,32,128]{4,3,2,1,0:T(8,128)} %get-tuple-element.24.p1, f32[4,16,2,32,128]{4,3,2,1,0:T(8,128)} %get-tuple-element.25.p2), custom_call_target="tpu_custom_call" | custom-call | tf_op jit(solution)/shard_map/pallas_call | solution.py:784
  (1 shorter events, 0.0 us)
Async XLA Ops:
  0.6 273.2 %copy-start.10 = (f32[8,32,16,128]{3,2,1,0:T(8,128)S(1)}, f32[8,32,16,128]{3,2,1,0:T(8,128)}, u32[]{:S(2)}) copy-start(f32[8,32,16,128]{3,2,1,0:T(8,128)} %right.3) | copy-start | bytes 6291460

commit v3 on v2

--- a/solution.py
+++ b/solution.py
@@ -11,10 +11,9 @@
 ITERS = 3
 SHIFT = 8.0
 SCALE = 8.0
-FLOOR = 3e-3
+FLOOR = 1e-2
 F32 = jnp.float32
 BF16 = jnp.bfloat16
-INTERPRET = False
 
 precise = lax.Precision.HIGHEST
 
@@ -57,50 +56,22 @@
     return both[:, size:]
 
 
-def least_pivots(matrix):
-    size = matrix.shape[0]
-    both = 0.5 * (matrix + matrix.T)
+def small(moments, columns):
+    span = ITERS * columns
+    pick = lambda first, count: moments[:, first * columns : first * columns + count]
+    both = jnp.concatenate([
+        jnp.concatenate((SHIFT * pick(j, span) + SCALE * pick(j + 1, span), pick(j, columns)), axis=1)
+        for j in range(ITERS)
+    ], axis=0)
     place = lax.broadcasted_iota(jnp.int32, both.shape, 0)
-    lane = lax.broadcasted_iota(jnp.int32, both.shape, 1)
-    for i in range(size):
-        row = both[i : i + 1] / both[i : i + 1, i : i + 1]
-        both = jnp.where(place > i, both - both[:, i : i + 1] * row, both)
-    return jnp.sum(jnp.where(place == lane, both, 0.0), axis=0, keepdims=True)
-
-
-def dot(left, right):
-    return jnp.dot(left, right, precision=precise, preferred_element_type=F32)
-
-
-def small(hankel):
-    columns = hankel.shape[0] // (ITERS + 1)
-
-    def operator(c):
-        zero = jnp.zeros((columns, columns), F32)
-        return SHIFT * c + SCALE * jnp.concatenate((zero, c[: ITERS * columns]), axis=0)
-
-    def inner(u, v):
-        return dot(u.T, dot(hankel, v))
-
-    shape = (hankel.shape[0], columns)
-    same = lax.broadcasted_iota(jnp.int32, shape, 0) == lax.broadcasted_iota(jnp.int32, shape, 1)
-    residual = jnp.where(same, 1.0, 0.0).astype(F32)
-    direction, answer = residual, jnp.zeros(shape, F32)
-    gamma = hankel[:columns, :columns]
-    start = least_pivots(gamma)
     fine = jnp.ones((1, columns), F32)
-    for iteration in range(ITERS):
-        image = operator(direction)
-        alpha = solve(inner(direction, image), gamma)
-        answer = answer + dot(direction, alpha)
-        if iteration + 1 < ITERS:
-            residual = residual - dot(image, alpha)
-            gamma_next = inner(residual, residual)
-            fine = jnp.where(least_pivots(gamma_next) > FLOOR * start, fine, 0.0)
-            beta = solve(gamma, gamma_next)
-            direction = residual + dot(direction, beta)
-            gamma = gamma_next
-    return answer, fine
+    old = both
+    for i in range(span):
+        pivot = both[i : i + 1, i : i + 1]
+        fine = jnp.where(pivot > FLOOR * old[i : i + 1, i : i + 1], fine, 0.0)
+        row = both[i : i + 1] / pivot
+        both = jnp.where(place == i, row, both - both[:, i : i + 1] * row)
+    return both[:, span:], fine
 
 
 def final_kernel(odd, c_ref, right, p1, p2, x_ref, g_ref):
@@ -164,7 +135,7 @@
                 barrier, inc=1, device_id=group.device(group.peer(step)), device_id_type=MESH
             )
             total += 1
-    pl.semaphore_wait(barrier, total)
+    return lambda: pl.semaphore_wait(barrier, total)
 
 
 def spread(group, source, target, send, recv):
@@ -186,7 +157,7 @@
 
 def total_kernel(sizes, v_ref, o_ref, part, one, two, send, recv, send2, recv2):
     slab, pencil = Group(sizes, "slab"), Group(sizes, "pencil")
-    greet((slab, pencil))
+    greet((slab, pencil))()
     part[...] = spread(pencil, v_ref, one, send, recv)
     o_ref[...] = spread(slab, part, two, send2, recv2)
 
@@ -204,8 +175,6 @@
 
 
 def total_of(matrix):
-    if INTERPRET:
-        return lax.psum(matrix, ("slab", "pencil"))
     sizes = {name: lax.axis_size(name) for name in ("slab", "pencil")}
     rows, columns = matrix.shape
     wide = jnp.pad(matrix, ((0, 0), (0, 128 - columns)))
@@ -242,6 +211,7 @@
     def brought(slot, src, dst):
         return pltpu.make_async_copy(src, dst, lsem.at[slot])
 
+    met = greet((slab, pencil))
     naturals = []
     for c in range(chunks):
         span = pl.ds(c * chunk, chunk)
@@ -256,7 +226,6 @@
     loads = [brought(4 * chunks + i, a, b) for i, (a, b) in enumerate(tables)]
     for load in loads:
         load.start()
-    greet((slab, pencil))
 
     def zrows(ref, y, count):
         return ref.at[:, pl.ds(y, count)]
@@ -505,9 +474,11 @@
 
     pieces = ys // piece
     early = max(pieces - 1, 1)
-    hop(0, 0)
     for c in range(chunks):
         turn(c)
+        if c == 0:
+            met()
+            hop(0, 0)
         for k in range(c * chunk // piece, (c + 1) * chunk // piece):
             if k < early:
                 start(zcopies(0, k, k * piece, piece, wa, w0))
@@ -559,15 +530,16 @@
     for slot, group in enumerate(groups):
         finish(zcopies(1, slot, *group, wa, x1))
     xfinish(5, [by_part(b) for b in range(blocks)])
-    for slot, group in enumerate(groups):
+    for group in [(row, chunk) for row in range(0, ys, chunk)]:
         absorb(5, group)
 
-        def leave(j, carry):
-            store(wa, group[0] + j, plane_back(j))
-            return carry
-
-        lax.fori_loop(0, group[1], leave, 0, unroll=YU)
-        start(zcopies(3, slot, *group, wa, x3))
+        for row in range(group[0], sum(group), piece):
+            def leave(j, carry):
+                store(wa, row + j, plane_back(row - group[0] + j))
+                return carry
+
+            lax.fori_loop(0, piece, leave, 0, unroll=YU)
+            start(zcopies(3, row // piece, row, piece, wa, x3))
 
     def tiles(step, row):
         y = row + step // depths
@@ -626,11 +598,11 @@
     for number, (l, r) in enumerate(((of0, of0), (of0, of1), (of1, of1), (of1, of2), (of2, of2))):
         moment(number, l, r)
     sums = zero
-    for slot, group in enumerate(groups):
-        finish(zcopies(3, slot, *group, wa, x3))
+    for k in range(pieces):
+        finish(zcopies(3, k, k * piece, piece, wa, x3))
 
         def last(step, sums):
-            y, z = tiles(step, group[0])
+            y, z = tiles(step, k * piece)
             mask = sown[y, z] * (1.0 / SCALE)
             factor = (nown[y, z] - SHIFT) * (1.0 / SCALE)
             lefts, rights = [], []
@@ -641,7 +613,7 @@
                 x3[place] = rights[-1]
             return tuple(s + lefts[i] * rights[j] for s, (i, j) in zip(sums, pairs))
 
-        sums = lax.fori_loop(0, group[1] * depths, last, sums)
+        sums = lax.fori_loop(0, piece * depths, last, sums)
     note(5, sums)
     out = pltpu.make_async_copy(x3, u2_o, lsem.at[2])
     out.start()
@@ -650,9 +622,7 @@
             left(number, stage)
     part_sum[...] = spread(pencil, stat, one, s1, r1)
     found = spread(slab, part_sum, two, s2, r2)
-    hankel = jnp.concatenate(
-        [found[:, j * columns : (j + ITERS + 1) * columns] for j in range(ITERS + 1)], axis=0)
-    c_ref[...], ok_ref[...] = small(hankel)
+    c_ref[...], ok_ref[...] = small(found, columns)
     finish(outs)
     out.wait()
 
@@ -670,10 +640,9 @@
     planes = (slabs, ys, 2, depth, nx)
     gathered = (slabs, ys, depth, nx)
     sent = (pencils, part, ys, wide)
-    groups = [(row, chunk) for row in range(0, ys, chunk)]
-    enter_groups = groups[:-1] + [
-        (row, piece) for row in range(groups[-1][0], ys, piece)
-    ]
+    whole_groups = [(row, chunk) for row in range(0, ys, chunk)]
+    enter_groups = whole_groups[:-1] + [(row, piece) for row in range(ys - chunk, ys, piece)]
+    groups = [(row, piece) for row in range(0, chunk, piece)] + whole_groups[1:]
     slots = max(len(enter_groups), len(groups), part // block)
     chunks = ys // chunk
     any_space = pl.BlockSpec(memory_space=pl.ANY)
@@ -703,7 +672,7 @@
         in_specs=[any_space] * 10,
         out_specs=(any_space, any_space, any_space, vmem, vmem),
         out_shape=(jax.ShapeDtypeStruct(planes, F32),) * 3 + (
-            jax.ShapeDtypeStruct(((ITERS + 1) * columns, columns), F32),
+            jax.ShapeDtypeStruct((ITERS * columns, columns), F32),
             jax.ShapeDtypeStruct((1, columns), F32),
         ),
         scratch_shapes=scratch,
@@ -714,16 +683,48 @@
     )(right, spectrum, noise, seen, *tables)
 
 
-def recurrences(p0, p1, p2, u2):
-    flat = lambda v: jnp.swapaxes(v, 1, 2).reshape(v.shape[0] * v.shape[2], -1)
-    basis = [flat(v) for v in (p0, p1, p2, u2)]
-    columns = basis[0].shape[0]
-
-    def field(c):
-        return sum(dot(c[k].T, basis[k]) for k in range(len(c)))
+def mixed_kernel(odd, u_ref, v_ref, p0, p1, p2, p3, o_ref):
+    quads, ys, _, depth, nx = p0.shape
+    columns = 2 * quads
+    tile = min(8, depth)
+    pairs = [(i, j) for i in range(columns) for j in range(i, columns)]
+
+    def body(step, sums):
+        y, z = step // (depth // tile), pl.ds(pl.multiple_of(step % (depth // tile) * tile, tile), tile)
+        tiles = [p0[i // 2, y, i % 2, z] for i in range(columns)]
+        for ref in (p1, p2, p3):
+            for i in range(columns):
+                tiles.append(ref[i, y, 0, z] if odd else ref[i // 2, y, i % 2, z])
+        left, right = (
+            [sum(t * c_ref[k, i] for k, t in enumerate(tiles)) for i in range(columns)]
+            for c_ref in (u_ref, v_ref)
+        )
+        return tuple(s + left[i] * right[j] for s, (i, j) in zip(sums, pairs))
+
+    zero = jnp.zeros((tile, nx), F32)
+    sums = lax.fori_loop(0, ys * (depth // tile), body, (zero,) * len(pairs))
+    for total, (i, j) in zip(sums, pairs):
+        row = jnp.sum(total, axis=0, keepdims=True)
+        o_ref[pl.ds(i * columns + j, 1)] = row
+        if i != j:
+            o_ref[pl.ds(j * columns + i, 1)] = row
+
+
+def recurrences(odd, basis):
+    columns = 2 * basis[0].shape[0]
 
     def gram(u, v):
-        return total_of(jnp.dot(u, v.T, precision=precise))
+        wide = [
+            jnp.pad(c.reshape(-1, columns), ((0, (ITERS + 1 - len(c)) * columns), (0, 0)))
+            for c in (u, v)
+        ]
+        rows = pl.pallas_call(
+            functools.partial(mixed_kernel, odd),
+            in_specs=[pl.BlockSpec(memory_space=pltpu.SMEM)] * 2
+            + [pl.BlockSpec(memory_space=pltpu.VMEM)] * 4,
+            out_shape=jax.ShapeDtypeStruct((columns * columns, basis[0].shape[-1]), F32),
+        )(*wide, *basis)
+        return total_of(jnp.sum(rows, axis=1).reshape(columns, columns))
 
     def operator(c):
         zero = jnp.zeros((1, columns, columns), F32)
@@ -734,16 +735,14 @@
 
     residual = direction = answer = jnp.eye(columns, dtype=F32)[None]
     answer = 0.0 * answer
-    vector = field(residual)
-    gamma = gram(vector, vector)
+    gamma = gram(residual, residual)
     for iteration in range(ITERS):
         image = operator(direction)
-        alpha = solve(gram(field(direction), field(image)), gamma)
+        alpha = solve(gram(direction, image), gamma)
         answer = answer + jnp.einsum("kij,jp->kip", direction, alpha, precision=precise)
         if iteration + 1 < ITERS:
             residual = longer(residual) - jnp.einsum("kij,jp->kip", image, alpha, precision=precise)
-            vector = field(residual)
-            gamma_next = gram(vector, vector)
+            gamma_next = gram(residual, residual)
             beta = solve(gamma, gamma_next)
             direction = residual + longer(
                 jnp.einsum("kij,jp->kip", direction, beta, precision=precise)
@@ -768,15 +767,10 @@
 
     def slow():
         field = jnp.transpose(right_sides.reshape(quads, 2, depth, ys, nx), (0, 3, 1, 2, 4))
-        basis = (p1, p2, u2)
-        if odd:
-            basis = [
-                jnp.swapaxes(v[:, :, 0].reshape(quads, 2, ys, depth, nx), 1, 2) for v in basis
-            ]
-        return recurrences(field, *basis)
+        return recurrences(odd, (field, p1, p2, u2))
 
     coefficients = lax.cond(
-        jnp.min(fine) > 0.5, lambda: coefficients[: 3 * columns], slow
+        jnp.min(fine) > 0.5, lambda: coefficients, slow
     )
     tile = min(8, depth)
     planes = pl.BlockSpec(p1.shape[:3] + (tile, nx), lambda i: (0, 0, 0, i, 0))

time: 282 us -> 274 us (0.972)
  Pallas kernels: 279 us -> 272 us
    pallas_call x1, Pallas kernels: 271 us -> 264 us  [krylov(): pl.pallas_call(functools.partial(krylov_kernel, sizes, (chunk, block, pie...]
where the time goes in v3:
time: 274 us
  Pallas kernels  272 us (99%)
    pallas_call x1, Pallas kernels, krylov(): pl.pallas_call(functools.partial(krylov_kernel, sizes, (chunk, block, pie...  264 us
    pallas_call x1, Pallas kernels, local(): pl.pallas_call(functools.partial(final_kernel, odd), grid=(depth // tile,...  7.27 us

profile of v3, /device:TPU:0, one launch (start us, length us, event | category | flops | bytes accessed | tf_op | source)
XLA Modules:
  0.0 274.1 jit_solution(17299687463951144766)
XLA Ops:
  0.6 264.3 %shard_map.113 = (f32[4,16,2,32,128]{4,3,2,1,0:T(8,128)S(1)}, f32[4,16,2,32,128]{4,3,2,1,0:T(8,128)}, f32[4,16,2,32,128]{4,3,2,1,0:T(8,128)}, f32[24,8]{1,0:T(8,128)S(1)}, f32[1,8]{1,0:T(1,128)}) custom-call(f32[8,32,16,128]{3,2,1,0:T(8,128)} %right.3, f32[16,32,128]{2,1,0:T(8,128)} %spectrum.1, f32[32,16,128]{2,1,0:T(8,128)} %noise.1, s32[32,16,128]{2,1,0:T(8,128)} %seen.1, ...), custom_call_target="tpu_custom_call" | custom-call | flops 8589934592 | bytes 67108864 | tf_op jit(solution)/shard_map/pallas_call | solution.py:669
  264.9 1.2 reduce_min.9
  266.8 7.3 %shard_map.114 = (f32[8,32,16,128]{3,2,1,0:T(8,128)}, f32[32,16,128]{2,1,0:T(8,128)}) custom-call(f32[24,8]{1,0:T(8,128)S(1)} %get-tuple-element.28.c_ref, f32[8,32,16,128]{3,2,1,0:T(8,128)} %right.3, f32[4,16,2,32,128]{4,3,2,1,0:T(8,128)S(1)} %get-tuple-element.24.p1, f32[4,16,2,32,128]{4,3,2,1,0:T(8,128)} %get-tuple-element.25.p2), custom_call_target="tpu_custom_call" | custom-call | tf_op jit(solution)/shard_map/pallas_call | solution.py:778
  (1 shorter events, 0.0 us)

commit v4 on v3

--- a/solution.py
+++ b/solution.py
@@ -252,7 +252,13 @@
         for copy in copies:
             copy.wait()
 
-    gathers = [(spectrum, lambda place: eig.at[place])]
+    gathers = []
+    for b in range(blocks):
+        span = pl.ds(b * block, block)
+        gathers.append((
+            spectrum.at[span], functools.partial(lambda span, place: eig.at[place, span], span)
+        ))
+    eigens = tuple(range(blocks))
     for c in range(chunks):
         span = pl.ds(c * chunk, chunk)
         for own, full in ((nown, noi), (sown, see)):
@@ -317,7 +323,7 @@
             relay(*numbers)
 
     def of_rows(c):
-        return (1 + 2 * c, 2 + 2 * c)
+        return (blocks + 2 * c, blocks + 2 * c + 1)
 
     def xcopy(number, slot, step, view):
         other = pencil.peer(step)
@@ -473,23 +479,21 @@
         lax.fori_loop(0, depths, body, 0)
 
     pieces = ys // piece
-    early = max(pieces - 1, 1)
+    met()
+    for number in eigens:
+        hop(number, 0)
     for c in range(chunks):
         turn(c)
-        if c == 0:
-            met()
-            hop(0, 0)
         for k in range(c * chunk // piece, (c + 1) * chunk // piece):
-            if k < early:
-                start(zcopies(0, k, k * piece, piece, wa, w0))
+            start(zcopies(0, k, k * piece, piece, wa, w0))
     own_loads = [
         brought(0, spectrum, eig.at[slab.me]), brought(1, nown, noi.at[slab.me]),
         brought(2, sown, see.at[slab.me]),
     ]
     start(own_loads)
-    relay(0)
-    for k in range(early, pieces):
-        start(zcopies(0, k, k * piece, piece, wa, w0))
+    relay(*eigens)
+    for number in of_rows(0):
+        hop(number, 0)
     for load in loads:
         load.wait()
     for slot, (row, count) in enumerate(enter_groups):
@@ -502,23 +506,17 @@
                 return carry
 
             lax.fori_loop(0, piece, enter, 0, unroll=YU)
-        if slot == max(len(enter_groups) - 2, 0):
-            relay(0)
-            for number in of_rows(0):
-                hop(number, 0)
         emit(0, slot, (row, count))
-    complete(0)
-    relay(*of_rows(0))
+    complete(*eigens)
     for c in range(1, chunks):
         for number in of_rows(c):
             hop(number, 0)
     finish(own_loads)
     xfinish(0, [by_rows(group) for group in enter_groups])
     middle(0)
-    for c in range(chunks):
-        relay(*of_rows(c))
-    for c in range(1, chunks):
-        relay(*of_rows(c))
+    for _ in range(2):
+        for c in range(chunks):
+            relay(*of_rows(c))
     xfinish(1, [by_part(b) for b in range(blocks)])
     advance(1, w0, wa, x1, 1, lambda c: complete(*of_rows(c)))
     xfinish(2, [by_rows(group) for group in groups])
@@ -622,7 +620,8 @@
             left(number, stage)
     part_sum[...] = spread(pencil, stat, one, s1, r1)
     found = spread(slab, part_sum, two, s2, r2)
-    c_ref[...], ok_ref[...] = small(found, columns)
+    c_ref[...], fine = small(found, columns)
+    ok_ref[0, 0] = jnp.min(fine)
     finish(outs)
     out.wait()
 
@@ -636,13 +635,14 @@
     wide = 2 * nz
     chunk = 8 if ys % 8 == 0 else ys
     block = min(4, part)
-    piece = min(4, chunk)
+    piece, half = min(2, chunk), max(chunk // 2, 1)
     planes = (slabs, ys, 2, depth, nx)
     gathered = (slabs, ys, depth, nx)
     sent = (pencils, part, ys, wide)
     whole_groups = [(row, chunk) for row in range(0, ys, chunk)]
-    enter_groups = whole_groups[:-1] + [(row, piece) for row in range(ys - chunk, ys, piece)]
-    groups = [(row, piece) for row in range(0, chunk, piece)] + whole_groups[1:]
+    enter_groups = whole_groups[:-1] + [(ys - chunk, chunk - half)]
+    enter_groups += [(row, piece) for row in range(ys - half, ys, piece)]
+    groups = [(row, half) for row in range(0, chunk, half)] + whole_groups[1:]
     slots = max(len(enter_groups), len(groups), part // block)
     chunks = ys // chunk
     any_space = pl.BlockSpec(memory_space=pl.ANY)
@@ -663,17 +663,17 @@
         + total_scratch(sizes, tile)[:3]
         + [dma((6, slots, pencils))] * 2 + [dma((6, slots))]
         + [dma((4, ys // piece, slabs))] * 2 + [dma((4, ys // piece))]
-        + [dma((1 + 2 * chunks, slabs, 2))] * 2 + [dma((4 * chunks + 6,))]
+        + [dma((part // block + 2 * chunks, slabs, 2))] * 2 + [dma((4 * chunks + 6,))]
         + total_scratch(sizes, tile)[3:]
     )
     return pl.pallas_call(
         functools.partial(krylov_kernel, sizes, (
             chunk, block, piece, slabs == columns, enter_groups, groups)),
         in_specs=[any_space] * 10,
-        out_specs=(any_space, any_space, any_space, vmem, vmem),
+        out_specs=(any_space,) * 3 + (vmem, pl.BlockSpec(memory_space=pltpu.SMEM)),
         out_shape=(jax.ShapeDtypeStruct(planes, F32),) * 3 + (
             jax.ShapeDtypeStruct((ITERS * columns, columns), F32),
-            jax.ShapeDtypeStruct((1, columns), F32),
+            jax.ShapeDtypeStruct((1, 1), F32),
         ),
         scratch_shapes=scratch,
         cost_estimate=pl.CostEstimate(flops=2**33, bytes_accessed=2**26, transcendentals=0),
@@ -770,16 +770,17 @@
         return recurrences(odd, (field, p1, p2, u2))
 
     coefficients = lax.cond(
-        jnp.min(fine) > 0.5, lambda: coefficients, slow
+        fine[0, 0] > 0.5, lambda: coefficients, slow
     )
     tile = min(8, depth)
-    planes = pl.BlockSpec(p1.shape[:3] + (tile, nx), lambda i: (0, 0, 0, i, 0))
-    natural = pl.BlockSpec((columns, tile, ys, nx), lambda i: (0, i, 0, 0))
+    rows = ys
+    planes = pl.BlockSpec((slabs, rows, 2, tile, nx), lambda i, j: (0, j, 0, i, 0))
+    natural = pl.BlockSpec((columns, tile, rows, nx), lambda i, j: (0, i, j, 0))
     return tuple(pl.pallas_call(
         functools.partial(final_kernel, odd),
-        grid=(depth // tile,),
+        grid=(depth // tile, ys // rows),
         in_specs=[pl.BlockSpec(memory_space=pltpu.SMEM), natural, planes, planes],
-        out_specs=(natural, pl.BlockSpec((tile, ys, nx), lambda i: (i, 0, 0))),
+        out_specs=(natural, pl.BlockSpec((tile, rows, nx), lambda i, j: (i, j, 0))),
         out_shape=(
             jax.ShapeDtypeStruct(right_sides.shape, F32),
             jax.ShapeDtypeStruct((depth, ys, nx), F32),

time: 274 us -> 272 us (level)
  no operation moved by 1% of the time
where the time goes in v4:
time: 272 us
  Pallas kernels  270 us (99%)
    pallas_call x1, Pallas kernels, krylov(): pl.pallas_call(functools.partial(krylov_kernel, sizes, (chunk, block, pie...  263 us
    pallas_call x1, Pallas kernels, local(): pl.pallas_call(functools.partial(final_kernel, odd), grid=(depth // tile,...  7.27 us

profile of v4, /device:TPU:0, one launch (start us, length us, event | category | flops | bytes accessed | tf_op | source)
XLA Modules:
  0.0 271.7 jit_solution(2446384240097222214)
XLA Ops:
  0.6 263.1 %shard_map.113 = (f32[4,16,2,32,128]{4,3,2,1,0:T(8,128)S(1)}, f32[4,16,2,32,128]{4,3,2,1,0:T(8,128)}, f32[4,16,2,32,128]{4,3,2,1,0:T(8,128)}, f32[24,8]{1,0:T(8,128)S(1)}, f32[1,1]{1,0:T(1,128)}) custom-call(f32[8,32,16,128]{3,2,1,0:T(8,128)} %right.3, f32[16,32,128]{2,1,0:T(8,128)} %spectrum.1, f32[32,16,128]{2,1,0:T(8,128)} %noise.1, s32[32,16,128]{2,1,0:T(8,128)} %seen.1, ...), custom_call_target="tpu_custom_call" | custom-call | flops 8589934592 | bytes 67108864 | tf_op jit(solution)/shard_map/pallas_call | solution.py:669
  264.4 7.3 %shard_map.114 = (f32[8,32,16,128]{3,2,1,0:T(8,128)}, f32[32,16,128]{2,1,0:T(8,128)}) custom-call(f32[24,8]{1,0:T(8,128)S(1)} %get-tuple-element.28.c_ref, f32[8,32,16,128]{3,2,1,0:T(8,128)} %right.3, f32[4,16,2,32,128]{4,3,2,1,0:T(8,128)S(1)} %get-tuple-element.24.p1, f32[4,16,2,32,128]{4,3,2,1,0:T(8,128)} %get-tuple-element.25.p2), custom_call_target="tpu_custom_call" | custom-call | tf_op jit(solution)/shard_map/pallas_call | solution.py:779
  (1 shorter events, 0.0 us)

commit v5 on v4

--- a/solution.py
+++ b/solution.py
@@ -634,7 +634,7 @@
     part, below, nz = spectrum.shape
     wide = 2 * nz
     chunk = 8 if ys % 8 == 0 else ys
-    block = min(4, part)
+    block = min(8, part)
     piece, half = min(2, chunk), max(chunk // 2, 1)
     planes = (slabs, ys, 2, depth, nx)
     gathered = (slabs, ys, depth, nx)

time: 272 us -> 270 us (level)
  no operation moved by 1% of the time
where the time goes in v5:
time: 270 us
  Pallas kernels  269 us (100%)
    pallas_call x1, Pallas kernels, krylov(): pl.pallas_call(functools.partial(krylov_kernel, sizes, (chunk, block, pie...  261 us
    pallas_call x1, Pallas kernels, local(): pl.pallas_call(functools.partial(final_kernel, odd), grid=(depth // tile,...  7.27 us

profile of v5, /device:TPU:0, one launch (start us, length us, event | category | flops | bytes accessed | tf_op | source)
XLA Modules:
  0.0 269.8 jit_solution(10458868833331414141)
XLA Ops:
  0.6 261.3 %shard_map.113 = (f32[4,16,2,32,128]{4,3,2,1,0:T(8,128)S(1)}, f32[4,16,2,32,128]{4,3,2,1,0:T(8,128)}, f32[4,16,2,32,128]{4,3,2,1,0:T(8,128)}, f32[24,8]{1,0:T(8,128)S(1)}, f32[1,1]{1,0:T(1,128)}) custom-call(f32[8,32,16,128]{3,2,1,0:T(8,128)} %right.3, f32[16,32,128]{2,1,0:T(8,128)} %spectrum.1, f32[32,16,128]{2,1,0:T(8,128)} %noise.1, s32[32,16,128]{2,1,0:T(8,128)} %seen.1, ...), custom_call_target="tpu_custom_call" | custom-call | flops 8589934592 | bytes 67108864 | tf_op jit(solution)/shard_map/pallas_call | solution.py:669
  262.6 7.3 %shard_map.114 = (f32[8,32,16,128]{3,2,1,0:T(8,128)}, f32[32,16,128]{2,1,0:T(8,128)}) custom-call(f32[24,8]{1,0:T(8,128)S(1)} %get-tuple-element.28.c_ref, f32[8,32,16,128]{3,2,1,0:T(8,128)} %right.3, f32[4,16,2,32,128]{4,3,2,1,0:T(8,128)S(1)} %get-tuple-element.24.p1, f32[4,16,2,32,128]{4,3,2,1,0:T(8,128)} %get-tuple-element.25.p2), custom_call_target="tpu_custom_call" | custom-call | tf_op jit(solution)/shard_map/pallas_call | solution.py:779
  (1 shorter events, 0.0 us)
